TPU v7x, 128 devices: a whole 4x4x4 slice. The times are simulated.
128 devices in a mesh: rep: 4 (over z_hi, core), row: 4 (over x), col: 8 (over z_lo, y).
Axes of the slice: x: 4, y: 4, z: 4 (z_hi: 2, z_lo: 2; z = z_hi * 2 + z_lo), core: 2. Of those that a mesh axis runs over, the one named last changes fastest.
Arguments:
- grad_parts: bfloat16 [4, 16384, 6144], P('rep', ('row', 'col')), may hold values from -0.03125 to 0.03125, as said below
- statistic: float32 [6144, 6144], P('row', 'col'), may hold values from -150 to 150, as said below
Outputs:
- gram_matrix: float32 [6144, 6144], P('row', 'col')
- statistic_next: float32 [6144, 6144], P('row', 'col')
Inputs may be any that keep to these rules, and one draw needn't show every extreme that they name: Every entry of grad_parts has a magnitude between 2^-10 and 2^-5. statistic is symmetric and positive definite.
All inputs are finite; a program needn't handle non-finite values.
Results may differ from a plain program's by a relative error of at most 0.008.
Values may be sent and summed in bfloat16 or wider, within the bound.
A program may use at most 128 MiB of HBM per device.

v0:
```python
import jax
import jax.numpy as jnp
from jax import lax
from jax.sharding import PartitionSpec as P


def shards(grad_parts, statistic):
    own_part = grad_parts[0].astype(jnp.float32)
    summed = lax.psum_scatter(own_part.astype(jnp.bfloat16), "rep", scatter_dimension=0, tiled=True)
    rows_panel = lax.all_to_all(summed, "row", split_axis=1, concat_axis=0, tiled=True)
    cols_panel = lax.all_to_all(summed, "col", split_axis=1, concat_axis=0, tiled=True)
    row_count = lax.axis_size("row")
    col_count = lax.axis_size("col")
    quarter = summed.shape[0]
    right_whole = lax.all_gather(cols_panel, "row", axis=0, tiled=True)
    right_order = (
        right_whole.reshape(row_count, col_count, quarter, -1)
        .transpose(1, 0, 2, 3)
        .reshape(row_count * col_count * quarter, -1)
    )
    partial_tile = lax.dot_general(
        lax.all_gather(rows_panel, "col", axis=0, tiled=True),
        right_order,
        (((0,), (0,)), ((), ())),
        preferred_element_type=jnp.float32,
    )
    portion = lax.psum_scatter(partial_tile, "rep", scatter_dimension=0, tiled=True)
    gram_tile = lax.all_gather(portion, "rep", axis=0, tiled=True)
    return (gram_tile, 0.95 * statistic + 0.05 * gram_tile)


def solution(mesh):
    return jax.shard_map(
        shards,
        mesh=mesh,
        in_specs=(P("rep", ("row", "col"), None), P("row", "col")),
        out_specs=(P("row", "col"), P("row", "col")),
        check_vma=False,
    )
```

profile of v0, /device:TPU:9, one launch (start us, length us, event | category | flops | bytes accessed | tf_op | source)
XLA Modules:
  0.0 440.4 jit_solution(476243138658292207)
XLA Ops:
  7.2 0.0 reduce-scatter.7.cloned.1.call-start
  7.2 0.7 reduce-scatter.7.cloned.1.call-update
  7.9 0.0 all-gather.6.cloned.1.call-start
  7.9 70.7 %reduce-scatter.7.cloned.1.call-done = bf16[128,6144]{1,0:T(8,128)(2,1)} async-done(((bf16[512,6144]{1,0:T(8,128)(2,1)}), bf16[128,6144]{1,0:T(8,128)(2,1)}) %reduce-scatter.7.cloned.1.call-update) | async-done | bytes 1572880
  78.7 1.9 copy.14
  80.6 23.7 %all_to_all.38 = bf16[128,8,768]{0,2,1:T(8,128)(2,1)S(1)} all-to-all(bf16[128,8,768]{0,2,1:T(8,128)(2,1)S(1)} %bitcast.15), channel_id=1, replica_groups=mesh['rep'=4,'row'=4,'col'=8] {'col'}, dimensions={1} | all-to-all | bytes 3145728 | tf_op jit(solution)/shard_map/all_to_all | solution.py:11
  104.3 1.6 copy.11
  105.9 0.0 all-gather.6.cloned.1.call-update
  105.9 0.0 all-gather.4.cloned.1.call-start
  106.0 28.9 %all_to_all.39 = bf16[128,4,1536]{0,2,1:T(8,128)(2,1)S(1)} all-to-all(bf16[128,4,1536]{0,2,1:T(8,128)(2,1)S(1)} %bitcast.16), channel_id=1, replica_groups=mesh['rep'=4,'row'=4,'col'=8] {'row'}, dimensions={1} | all-to-all | bytes 3145728 | tf_op jit(solution)/shard_map/all_to_all | solution.py:10
  134.9 1.6 copy.10
  136.5 0.0 all-gather.4.cloned.1.call-update
  136.5 0.0 reduce-scatter.5.cloned.1.call-start
  136.5 45.0 %all-gather.6.cloned.1.call-done = bf16[4096,768]{1,0:T(8,128)(2,1)} async-done(((bf16[1024,768]{1,0:T(8,128)(2,1)}), bf16[4096,768]{1,0:T(8,128)(2,1)}) %all-gather.6.cloned.1.call-update) | async-done | bytes 6291472 | tf_op jit(solution)/shard_map/all_gather | solution.py:15
  181.5 6.0 %copy.12 = bf16[4,8,128,768]{3,2,0,1:T(8,128)(2,1)} copy(bf16[4,8,128,768]{3,2,1,0:T(8,128)(2,1)} %bitcast.18) | data formatting | bytes 12582912 | tf_op jit(solution)/shard_map/reshape | solution.py:17
  187.5 121.8 %all-gather.4.cloned.1.call-done = bf16[4096,1536]{1,0:T(8,128)(2,1)} async-done(((bf16[512,1536]{1,0:T(8,128)(2,1)}), bf16[4096,1536]{1,0:T(8,128)(2,1)}) %all-gather.4.cloned.1.call-update) | async-done | bytes 12582928 | tf_op jit(solution)/shard_map/all_gather | solution.py:22
  309.4 16.3 %fusion = f32[1536,768]{1,0:T(8,128)} fusion(bf16[4096,1536]{1,0:T(8,128)(2,1)} %all-gather.4.cloned.1.call-done, bf16[4096,768]{1,0:T(8,128)(2,1)} %bitcast.19), kind=kOutput, calls=%fused_computation.1 | convolution fusion | flops 9663676416 | bytes 23592960 | tf_op jit(solution)/shard_map/dot_general | solution.py:21
  325.7 0.0 reduce-scatter.5.cloned.1.call-update
  325.8 0.0 all-gather.8.cloned.1.call-start
  325.8 56.1 %reduce-scatter.5.cloned.1.call-done = f32[384,768]{1,0:T(8,128)} async-done(((f32[1536,768]{1,0:T(8,128)}), f32[384,768]{1,0:T(8,128)}) %reduce-scatter.5.cloned.1.call-update) | async-done | bytes 1179664 | tf_op jit(solution)/shard_map/reduce_scatter | solution.py:27
  381.9 0.0 all-gather.8.cloned.1.call-update
  381.9 42.9 %all-gather.8.cloned.1.call-done = f32[1536,768]{1,0:T(8,128)} async-done(((f32[384,768]{1,0:T(8,128)}), f32[1536,768]{1,0:T(8,128)}) %all-gather.8.cloned.1.call-update) | async-done | bytes 4718608 | tf_op jit(solution)/shard_map/all_gather | solution.py:28
  424.8 0.0 copy-start
  424.8 6.8 %multiply_add_fusion = f32[1536,768]{1,0:T(8,128)} fusion(f32[1536,768]{1,0:T(8,128)} %all-gather.8.cloned.1.call-done, f32[1536,768]{1,0:T(8,128)} %param.3), kind=kLoop, calls=%fused_computation | loop fusion | flops 3538944 | bytes 14155776 | tf_op jit(solution)/shard_map/add | solution.py:29
  431.7 0.0 copy-done
  431.7 2.2 copy.17
Async XLA Ops:
  7.2 71.5 %reduce-scatter.7.cloned.1.call-start = ((), (), s32[]{:S(2)}) async-start(), calls=%async_computation.8 | async-start | bytes 7864320
  7.9 173.6 %all-gather.6.cloned.1.call-start = ((), (), s32[]{:S(2)}) async-start(), calls=%async_computation.5 | async-start | bytes 7864320 | tf_op jit(solution)/shard_map/all_gather | solution.py:15
  105.9 203.5 %all-gather.4.cloned.1.call-start = ((), (), s32[]{:S(2)}) async-start(), calls=%async_computation.4 | async-start | bytes 14155776 | tf_op jit(solution)/shard_map/all_gather | solution.py:22
  136.5 245.4 %reduce-scatter.5.cloned.1.call-start = ((), (), s32[]{:S(2)}) async-start(), calls=%async_computation.6 | async-start | bytes 5898240 | tf_op jit(solution)/shard_map/reduce_scatter | solution.py:27
  325.8 99.1 %all-gather.8.cloned.1.call-start = ((), (), s32[]{:S(2)}) async-start(), calls=%async_computation.7 | async-start | bytes 5898240 | tf_op jit(solution)/shard_map/all_gather | solution.py:28
  424.8 6.9 %copy-start = (f32[1536,768]{1,0:T(8,128)S(1)}, f32[1536,768]{1,0:T(8,128)}, u32[]{:S(2)}) copy-start(f32[1536,768]{1,0:T(8,128)} %all-gather.8.cloned.1.call-done) | copy-start | bytes 14155780
Sparse Core Ops, SparseCore 0:
  10.6 68.0 reduce-scatter.6
  106.0 75.4 all-gather.5
  183.7 125.6 all-gather.3
  325.9 55.9 reduce-scatter.4
  383.4 41.3 all-gather.7
where the time goes:
time: 442 us; the launch traced here: 440 us
  waiting for transfers between devices  337 us (76%)
  blocking collectives  52.7 us (12%)
  matrix products  16.3 us (4%)
  between operations  13.8 us (3%)
  local copies, waits for them, and re-layouts  13.3 us (3%)
  other arithmetic  6.85 us (2%)
    all_gather x1, waiting for transfers between devices, shards(): lax.all_gather(rows_panel, 'col', axis=0, tiled=True)  122 us
    unnamed x6, waiting for transfers between devices  71.5 us
    reduce_scatter x1, waiting for transfers between devices, shards(): lax.psum_scatter(partial_tile, 'rep', scatter_dimension=0, tiled=True)  56.1 us
    all_gather x1, waiting for transfers between devices, shards(): right_whole = lax.all_gather(cols_panel, 'row', axis=0, tiled=True)  45 us
    all_gather x1, waiting for transfers between devices, shards(): gram_tile = lax.all_gather(portion, 'rep', axis=0, tiled=True)  42.9 us
    all_to_all x1, blocking collectives, shards(): lax.all_to_all(summed, 'row', split_axis=1, concat_axis=0, tiled=True)  28.9 us
    all_to_all x1, blocking collectives, shards(): lax.all_to_all(summed, 'col', split_axis=1, concat_axis=0, tiled=True)  23.7 us
    dot_general x1, matrix products, shards(): lax.dot_general(lax.all_gather(rows_panel, 'col', axis=0, tiled=True), ri...  16.3 us
  transfers between devices with their start and end apart: 5, of which 5 were waited for; matrix products, arithmetic and copies ran while one was open for 2% of the time, Pallas kernels for 0%

commit v1 on v0

v1 whole, which is shorter than its diff:
```python
import functools

import jax
import jax.numpy as jnp
from jax import lax
from jax.experimental import pallas as pl
from jax.experimental.pallas import tpu as pltpu
from jax.sharding import PartitionSpec as P

MESH = pl.DeviceIdType.MESH
BF16 = jnp.bfloat16
F32 = jnp.float32
CHUNKS = 16


def mod(a, n):
    return lax.rem(a, n)


def rcopy(src, dst, send, recv, device):
    return pltpu.make_async_remote_copy(
        src_ref=src, dst_ref=dst, send_sem=send, recv_sem=recv, device_id=device, device_id_type=MESH
    )


class Ring:
    def __init__(self, i, up, down, src, add, bufs, sends, recvs):
        self.i, self.src, self.add = i, src, add
        (ra, rb, fa, fb, ga, gb, sa, sb) = bufs
        at = lambda j: mod(i + j, 4)
        mk = lambda n, s, d, dev: rcopy(s, d, sends.at[n], recvs.at[n], dev)
        self.sa, self.sb, self.at = sa, sb, at
        self.ra = mk(0, src(0, at(2)), ra, up)
        self.rb = mk(1, src(1, at(2)), rb, down)
        self.fb = mk(2, src(1, at(1)), fb, up)
        self.fa = mk(3, src(0, at(3)), fa, down)
        self.ga = mk(4, sa, ga, up)
        self.gb = mk(5, sb, gb, down)
        self.bufs = bufs

    def far(self):
        self.ra.start()
        self.rb.start()

    def near_up(self):
        self.fb.start()

    def near_down(self):
        self.fa.start()

    def pass_on(self):
        ra, rb = self.bufs[0], self.bufs[1]
        self.ra.wait_recv()
        self.sa[...] = (ra[...].astype(F32) + self.add(0, self.at(1))).astype(BF16)
        self.ga.start()
        self.rb.wait_recv()
        self.sb[...] = (rb[...].astype(F32) + self.add(1, self.at(3))).astype(BF16)
        self.gb.start()

    def result(self):
        _, _, fa, fb, ga, gb, _, _ = self.bufs
        self.fa.wait_recv()
        self.ga.wait_recv()
        a = self.add(0, self.i) + (fa[...].astype(F32) + ga[...].astype(F32))
        self.fb.wait_recv()
        self.gb.wait_recv()
        b = self.add(1, self.i) + (fb[...].astype(F32) + gb[...].astype(F32))
        return a, b

    def drain(self):
        for c in (self.ra, self.rb, self.fb, self.fa, self.ga, self.gb):
            c.wait_send()


def kernel(
    g, out, gown, gsib, psend, zrel, zrec, sline, t, u,
    al, be, t8a, t8b, a2, b2, c2a, c2b, xf, xb, x8f, x8b, zf, zb, oa, o8,
    lsem, csend, crecv, rsend, rrecv, fsend, frecv, dsend, drecv,
):
    rep, x, col = lax.axis_index("rep"), lax.axis_index("row"), lax.axis_index("col")
    zh, k = lax.div(rep, 2), mod(rep, 2)
    zl, y = lax.div(col, 4), mod(col, 4)
    z = 2 * zh + zl
    q, d = psend.shape
    half = q // 2
    w = d // CHUNKS
    b = d // 8
    h = b // 2
    hq = h // 4
    h8 = hq // 2

    def dev(x, y, z, k):
        return {"rep": lax.div(z, 2) * 2 + k, "row": x, "col": mod(z, 2) * 4 + y}

    sib = dev(x, y, z, 1 - k)
    zp, zm = dev(x, y, mod(z + 1, 4), k), dev(x, y, mod(z + 3, 4), k)
    yp, ym = dev(x, mod(y + 1, 4), z, k), dev(x, mod(y + 3, 4), z, k)
    xp, xm = dev(mod(x + 1, 4), y, z, k), dev(mod(x + 3, 4), y, z, k)

    def cols(c):
        return pl.ds(pl.multiple_of(c * w, w), w)

    def rows(i):
        return pl.ds(pl.multiple_of(i * q, q), q)

    def load(c):
        return pltpu.make_async_copy(g.at[:, k, :, cols(c)], gown.at[:, :, cols(c)], lsem.at[c])

    def swap(c):
        return rcopy(g.at[:, 1 - k, :, cols(c)], gsib.at[:, :, cols(c)], csend.at[0], crecv.at[0, c], sib)

    def z1(c):
        return (
            rcopy(psend.at[0:half, cols(c)], zrel.at[0, :, cols(c)], csend.at[1], crecv.at[1, c], zp),
            rcopy(psend.at[half:q, cols(c)], zrel.at[1, :, cols(c)], csend.at[2], crecv.at[2, c], zm),
        )

    def z2(c):
        return (
            rcopy(zrel.at[0, :, cols(c)], zrec.at[0, :, cols(c)], csend.at[3], crecv.at[3, c], zp),
            rcopy(zrel.at[1, :, cols(c)], zrec.at[1, :, cols(c)], csend.at[4], crecv.at[4, c], zm),
        )

    def block(j, c, part=None):
        base = (2 * mod(y + j, 4) + k) * q
        if part is None:
            return sline.at[pl.ds(pl.multiple_of(base, q), q), cols(c)]
        return sline.at[pl.ds(pl.multiple_of(base + part * half, half), half), cols(c)]

    def sblock(j, c):
        return sline.at[pl.ds(pl.multiple_of((2 * mod(y + j, 4) + 1 - k) * q, q), q), cols(c)]

    def y1(c):
        own = block(0, c)
        return (
            rcopy(own, own, csend.at[5], crecv.at[5, c], yp),
            rcopy(own, own, csend.at[6], crecv.at[6, c], ym),
        )

    def y1_landed(c):
        down, upper = block(3, c), block(1, c)
        return (
            rcopy(down, down, csend.at[5], crecv.at[5, c], yp),
            rcopy(upper, upper, csend.at[6], crecv.at[6, c], ym),
        )

    def y2(c):
        down, upper = block(3, c, 0), block(1, c, 1)
        return (
            rcopy(down, down, csend.at[7], crecv.at[7, c], yp),
            rcopy(upper, upper, csend.at[8], crecv.at[8, c], ym),
        )

    def y2_landed(c):
        lo, hi = block(2, c, 0), block(2, c, 1)
        return (
            rcopy(lo, lo, csend.at[7], crecv.at[7, c], yp),
            rcopy(hi, hi, csend.at[8], crecv.at[8, c], ym),
        )

    def share(j, c):
        blk = block(j, c)
        return rcopy(blk, blk, csend.at[9 + j], crecv.at[9 + j, c], sib)

    def share_landed(j, c):
        blk = sblock(j, c)
        return rcopy(blk, blk, csend.at[9 + j], crecv.at[9 + j, c], sib)

    @pl.loop(0, CHUNKS)
    def _(c):
        load(c).start()
        swap(c).start()

    @pl.loop(0, CHUNKS + 4)
    def _(step):
        @pl.when(step < CHUNKS)
        def _():
            c = step
            load(c).wait()
            swap(c).wait_recv()
            o = 1 - zh
            psend[:, cols(c)] = (gown[o, :, cols(c)].astype(F32) + gsib[o, :, cols(c)].astype(F32)).astype(BF16)
            for cp in z1(c):
                cp.start()

        @pl.when((step >= 1) & (step < CHUNKS + 1))
        def _():
            c = step - 1
            for cp, fwd in zip(z1(c), z2(c)):
                cp.wait_recv()
                fwd.start()

        @pl.when((step >= 2) & (step < CHUNKS + 2))
        def _():
            c = step - 2
            for cp in z2(c):
                cp.wait_recv()
            own = gown[zh, :, cols(c)].astype(F32) + gsib[zh, :, cols(c)].astype(F32)
            far = jnp.concatenate([zrec[0, :, cols(c)], zrec[1, :, cols(c)]], axis=0).astype(F32)
            sline[rows(2 * y + k), cols(c)] = (own + far).astype(BF16)
            for cp in y1(c):
                cp.start()
            share(0, c).start()

        @pl.when((step >= 3) & (step < CHUNKS + 3))
        def _():
            c = step - 3
            for cp, fwd, j in zip(y1_landed(c), y2(c), (3, 1)):
                cp.wait_recv()
                fwd.start()
                share(j, c).start()

        @pl.when(step >= 4)
        def _():
            c = step - 4
            for cp in y2_landed(c):
                cp.wait_recv()
            share(2, c).start()

    @pl.loop(0, CHUNKS)
    def _(c):
        for j in range(4):
            share_landed(j, c).wait_recv()

    def sent(n, ref):
        rcopy(ref, ref, csend.at[n], crecv.at[0, 0], sib).wait_send()

    sent(0, gsib)
    for n in (1, 2, 3, 4):
        sent(n, zrel.at[0])
    for n in (5, 6, 9, 10, 11, 12):
        sent(n, psend)
    for n in (7, 8):
        sent(n, zrel.at[0])

    def cof(r):
        return y + 4 * lax.div(mod(r - y + 8, 8), 4)

    def tile(slot, r, c):
        lhs = sline[:, pl.ds(pl.multiple_of(r * b + k * h, h), h)]
        rhs = sline[:, pl.ds(pl.multiple_of(c * b, b), b)]
        acc = lax.dot_general(lhs, rhs, (((0,), (0,)), ((), ())), preferred_element_type=F32)
        t[slot] = acc.astype(BF16)

    def pair(j):
        @pl.loop(0, 2)
        def _(s):
            r = 2 * mod(x + j, 4) + s
            tile(r, r, cof(r))

    def hrows(i, n):
        return pl.ds(pl.multiple_of(i * n, n), n)

    f = lambda v: v.astype(F32)
    left, right = slice(0, h), slice(h, b)
    xring = lambda n, src, add, bufs: Ring(x, xp, xm, src, add, bufs, rsend.at[n], rrecv.at[n])
    zring = lambda n, src, add, bufs: Ring(z, zp, zm, src, add, bufs, rsend.at[n], rrecv.at[n])

    alpha = xring(
        0,
        lambda s, p: t.at[2 * p + s, :, left],
        lambda s, p: f(t[2 * p + s, :, left]),
        [al.at[n] for n in range(8)],
    )
    eight = xring(
        1,
        lambda s, p: t.at[8, hrows(p, hq), (left, right)[s]],
        lambda s, p: f(t[8, hrows(p, hq), (left, right)[s]]),
        [t8a.at[n] for n in range(8)],
    )

    def beta_of(j):
        p = mod(x + j, 4)
        return zring(
            2 + j,
            lambda s, v: t.at[2 * p + s, hrows(v, hq), right],
            lambda s, v: f(t[2 * p + s, hrows(v, hq), right]),
            [be.at[j, n] for n in range(8)],
        )

    beta = [beta_of(j) for j in range(4)]

    def start_all(ring):
        ring.far()
        ring.near_up()
        ring.near_down()

    pair(2)
    alpha.far()
    start_all(beta[2])
    pair(1)
    alpha.near_up()
    start_all(beta[1])
    pair(3)
    alpha.near_down()
    start_all(beta[3])
    tile(8, y, y + 4)
    start_all(eight)
    pair(0)
    start_all(beta[0])
    alpha.pass_on()
    beta[2].pass_on()
    eight.pass_on()
    for j in (1, 3, 0):
        beta[j].pass_on()

    beta2 = xring(
        6, lambda s, p: zb.at[2 * p + s], lambda s, p: zf[2 * p + s], [b2.at[n] for n in range(8)]
    )
    alpha2 = zring(
        7,
        lambda s, v: xb.at[s, hrows(v, hq), :],
        lambda s, v: xf[s, hrows(v, hq), :],
        [a2.at[n] for n in range(8)],
    )
    ha = 2 * h // 3
    eight_cols = (slice(0, ha), slice(ha, h))

    def piece8(v):
        return hrows(lax.div(v, 2), h8), mod(v, 2)

    def src8(s, v):
        r, c = piece8(v)
        return x8b.at[c, r, eight_cols[s]]

    def add8(s, v):
        r, c = piece8(v)
        return x8f[c, r, eight_cols[s]]

    bufs8 = [(c2a, c2b)[n % 2].at[n // 2] for n in range(8)]
    eight2 = zring(8, src8, add8, bufs8)

    for j, go in ((2, beta2.far), (1, beta2.near_up), (3, beta2.near_down), (0, None)):
        for s, v in enumerate(beta[j].result()):
            zf[2 * mod(x + j, 4) + s] = v
            zb[2 * mod(x + j, 4) + s] = v.astype(BF16)
        if go is not None:
            go()
    for s, v in enumerate(alpha.result()):
        xf[s] = v
        xb[s] = v.astype(BF16)
    start_all(alpha2)
    for s, v in enumerate(eight.result()):
        x8f[s] = v
        x8b[s] = v.astype(BF16)
    start_all(eight2)
    beta2.pass_on()
    alpha2.pass_on()
    eight2.pass_on()
    for s, v in enumerate(beta2.result()):
        oa[s, :, right] = v.astype(BF16)
    for s, v in enumerate(alpha2.result()):
        oa[s, :, left] = v.astype(BF16)
    for s, v in enumerate(eight2.result()):
        o8[:, eight_cols[s]] = v.astype(BF16)

    place = pl.ds(pl.multiple_of(k * h + z * hq, hq), hq)
    place8 = pl.ds(pl.multiple_of(k * h + x * hq + lax.div(z, 2) * h8, h8), h8)
    cols8 = pl.ds(pl.multiple_of(mod(z, 2) * h, h), h)

    def to_direct(s, up, act):
        r = 2 * x + s
        c = cof(r)
        to = 2 * up + lax.div(c, 4)
        src, dst = oa.at[s], u.at[s, place, :]

        @pl.when(to != z)
        def _():
            act(rcopy(src, dst, fsend.at[s, up], frecv.at[s], dev(x, y, to, k)))

        return to == z, src, dst

    def to_mirror(s, up, act):
        r = 2 * x + s
        c = cof(r)

        @pl.when(r != c)
        def _():
            slot = mod(c, 2)
            to = dev(lax.div(c, 2), mod(r, 4), 2 * up + lax.div(r, 4), k)
            act(rcopy(oa.at[s], u.at[slot, place, :], fsend.at[s, 2 + up], frecv.at[slot], to))

    def to_eight(side, up, act):
        slot = mod(y, 2)
        tx, tz = lax.div(y + 4 * side, 2), 2 * up + 1 - side
        src, dst = o8, u.at[slot, place8, cols8]

        @pl.when((tx != x) | (tz != z))
        def _():
            act(rcopy(src, dst, fsend.at[2, 2 * side + up], frecv.at[slot], dev(tx, y, tz, k)))

        return (tx == x) & (tz == z), src, dst

    begin = lambda cp: cp.start()
    ended = lambda cp: cp.wait_send()
    for up in (0, 1):
        for s in (0, 1):
            mine, src, dst = to_direct(s, up, begin)

            @pl.when(mine)
            def _():
                pltpu.make_async_copy(src, dst, frecv.at[s]).start()

            to_mirror(s, up, begin)
        for side in (0, 1):
            mine, src, dst = to_eight(side, up, begin)

            @pl.when(mine)
            def _():
                pltpu.make_async_copy(src, dst, frecv.at[mod(y, 2)]).start()

    for ring in (alpha, eight, *beta, beta2, alpha2, eight2):
        ring.drain()

    for s in (0, 1):
        part = u.at[s, hrows(k, h), :]
        rcopy(part, part, fsend.at[s, 0], frecv.at[s], sib).wait_recv()
        rcopy(part, part, dsend.at[s], drecv.at[s], sib).start()
    for up in (0, 1):
        for s in (0, 1):
            to_direct(s, up, ended)
            to_mirror(s, up, ended)
        for side in (0, 1):
            to_eight(side, up, ended)
    for s in (0, 1):
        part, other = u.at[s, hrows(k, h), :], u.at[s, hrows(1 - k, h), :]
        rcopy(other, other, dsend.at[s], drecv.at[s], sib).wait_recv()
        rcopy(part, part, dsend.at[s], drecv.at[s], sib).wait_send()
        pltpu.make_async_copy(u.at[s], out.at[s], lsem.at[s]).start()
    for s in (0, 1):
        pltpu.make_async_copy(u.at[s], out.at[s], lsem.at[s]).wait()


def gather_tiles(grad):
    _, n, d = grad.shape
    q, b = n // 4, d // 8
    h = b // 2
    hq = h // 4
    h8 = hq // 2
    ha = 2 * h // 3
    vm = pltpu.VMEM
    dma = pltpu.SemaphoreType.DMA
    return pl.pallas_call(
        kernel,
        out_shape=jax.ShapeDtypeStruct((2, b, b), BF16),
        in_specs=[pl.BlockSpec(memory_space=pl.ANY)],
        out_specs=pl.BlockSpec(memory_space=pl.ANY),
        scratch_shapes=[
            vm((2, q, d), BF16), vm((2, q, d), BF16), vm((q, d), BF16),
            vm((2, q // 2, d), BF16), vm((2, q // 2, d), BF16),
            vm((8 * q, d), BF16), vm((9, h, b), BF16), vm((2, b, b), BF16),
            vm((8, h, h), BF16), vm((4, 8, hq, h), BF16), vm((8, hq, h), BF16), vm((8, hq, h), BF16),
            vm((8, hq, h), BF16), vm((8, hq, h), BF16), vm((4, h8, ha), BF16), vm((4, h8, h - ha), BF16),
            vm((2, h, h), F32), vm((2, h, h), BF16), vm((2, hq, h), F32), vm((2, hq, h), BF16),
            vm((8, hq, h), F32), vm((8, hq, h), BF16), vm((2, hq, b), BF16), vm((h8, h), BF16),
            dma((CHUNKS,)), dma((13,)), dma((13, CHUNKS)), dma((9, 6)), dma((9, 6)),
            dma((3, 4)), dma((2,)), dma((2,)), dma((2,)),
        ],
        compiler_params=pltpu.CompilerParams(has_side_effects=True, vmem_limit_bytes=64 * 1024 * 1024 - 66 * 1024),
    )(grad.reshape(2, 2, q, d))


def shards(grad, statistic):
    tiles = gather_tiles(grad)
    x, col = lax.axis_index("row"), lax.axis_index("col")
    parts = []
    for s in (0, 1):
        r = 2 * x + s
        apart = (r - col) % 8
        mirrored = (apart > 4) | ((apart == 4) & (r >= 4))
        parts.append(jnp.where(mirrored, tiles[s].T, tiles[s]).astype(F32))
    gram = jnp.concatenate(parts, axis=0)
    return gram, 0.95 * statistic + 0.05 * gram


def solution(mesh):
    return jax.shard_map(
        shards,
        mesh=mesh,
        in_specs=(P("rep", ("row", "col"), None), P("row", "col")),
        out_specs=(P("row", "col"), P("row", "col")),
        check_vma=False,
    )
```

time: 442 us -> 166 us (0.38)
  the two profiles are of different devices: /device:TPU:9 before, /device:TPU:79 now
where the time goes in v1:
time: 166 us
  Pallas kernels  149 us (90%)
  other arithmetic  8.84 us (5%)
  local copies, waits for them, and re-layouts  6.76 us (4%)
    pallas_call x1, Pallas kernels, gather_tiles(): pl.pallas_call(kernel, out_shape=jax.ShapeDtypeStruct((2, b, b), BF16), i...  149 us
    add x1, other arithmetic, shards(): return (gram, 0.95 * statistic + 0.05 * gram)  6.99 us
    transpose x2, local copies, waits for them, and re-layouts, shards(): parts.append(jnp.where(mirrored, tiles[s].T, tiles[s]).astype(F32))  5.31 us

profile of v1, /device:TPU:79, one launch (start us, length us, event | category | flops | bytes accessed | tf_op | source)
XLA Modules:
  0.0 165.5 jit_solution(2600453386835912023)
XLA Ops:
  0.7 149.2 %shard_map.41 = bf16[2,768,768]{2,1,0:T(8,128)(2,1)} custom-call(bf16[2,2,128,6144]{3,2,1,0:T(8,128)(2,1)} %bitcast.12), custom_call_target="tpu_custom_call" | custom-call | tf_op jit(solution)/shard_map/pallas_call | solution.py:443
  149.9 2.8 %slice_bitcast_fusion.1 = (bf16[768,768]{0,1:T(8,128)(2,1)}, bf16[768,768]{1,0:T(8,128)(2,1)S(1)}) fusion(bf16[2,768,768]{2,1,0:T(8,128)(2,1)} %shard_map.41), kind=kLoop, calls=%fused_computation.5 | loop fusion | bytes 4718592 | tf_op jit(solution)/shard_map/transpose | solution.py:471
  152.7 0.0 copy-start
  152.7 2.5 %copy.4 = bf16[768,768]{1,0:T(8,128)(2,1)} copy(bf16[768,768]{0,1:T(8,128)(2,1)} %get-tuple-element.6) | data formatting | bytes 2359296 | tf_op jit(solution)/shard_map/transpose | solution.py:471
  155.2 1.4 copy.5
  156.7 0.0 copy-done
  156.7 1.9 %bitcast_select_fusion.1 = (bf16[768,768]{1,0:T(8,128)(2,1)S(1)}, bf16[768,768]{1,0:T(8,128)(2,1)S(1)}) fusion(bf16[768,768]{1,0:T(8,128)(2,1)} %copy.4, pred[]{:T(512)S(6)} %or.6, bf16[2,768,768]{2,1,0:T(8,128)(2,1)S(1)} %copy-done, bf16[768,768]{0,1:T(8,128)(2,1)} %copy.5, pred[]{:T(512)S(6)} %or.7), kind=kLoop, calls=%fused_computation.3 | loop fusion | flops 1179648 | bytes 7077890 | tf_op jit(solution)/shard_map/jit(_where)/select_n | solution.py:471
  158.5 7.0 %multiply_add_fusion = (f32[1536,768]{1,0:T(8,128)}, f32[1536,768]{1,0:T(8,128)}) fusion(f32[1536,768]{1,0:T(8,128)} %param.3, bf16[768,768]{1,0:T(8,128)(2,1)S(1)} %get-tuple-element.5, bf16[768,768]{1,0:T(8,128)(2,1)S(1)} %get-tuple-element.4), kind=kLoop, calls=%fused_computation | loop fusion | flops 8257536 | bytes 16515072 | tf_op jit(solution)/shard_map/add | solution.py:473
Async XLA Ops:
  152.7 4.0 %copy-start = (bf16[2,768,768]{2,1,0:T(8,128)(2,1)S(1)}, bf16[2,768,768]{2,1,0:T(8,128)(2,1)}, u32[]{:S(2)}) copy-start(bf16[2,768,768]{2,1,0:T(8,128)(2,1)} %shard_map.41) | copy-start | bytes 7077892

commit v2 on v0

v2 whole, which is shorter than its diff:
```python
import functools

import jax
import jax.numpy as jnp
from jax import lax
from jax.experimental import pallas as pl
from jax.experimental.pallas import tpu as pltpu
from jax.sharding import PartitionSpec as P

MESH = pl.DeviceIdType.MESH
BF16 = jnp.bfloat16
F32 = jnp.float32
STAGES = 6
PER = 2
CHUNKS = STAGES * PER


def mod(a, n):
    return lax.rem(a, n)


def rcopy(src, dst, send, recv, device):
    return pltpu.make_async_remote_copy(
        src_ref=src, dst_ref=dst, send_sem=send, recv_sem=recv, device_id=device, device_id_type=MESH
    )


class Ring:
    def __init__(self, i, up, down, n, src, add, bufs, sends, recvs):
        self.i, self.n, self.add = i, n, add
        (ra, rb, fa, fb, ga, gb, sa, sb) = bufs
        at = lambda j: mod(i + j, 4)
        mk = lambda n, s, d, dev: rcopy(s, d, sends.at[n], recvs.at[n], dev)
        self.at = at
        self.ra = mk(0, src(0, at(2)), ra, up)
        self.rb = mk(1, src(1, at(2)), rb, down)
        self.fb = mk(2, src(1, at(1)), fb, up)
        self.fa = mk(3, src(0, at(3)), fa, down)
        self.ga = mk(4, sa, ga, up)
        self.gb = mk(5, sb, gb, down)
        self.bufs = bufs

    def start(self):
        self.ra.start()
        self.rb.start()
        self.fb.start()
        self.fa.start()

    def pass_on(self):
        ra, rb, _, _, _, _, sa, sb = self.bufs
        for far, got, sum_, s, to, on in ((self.ra, ra, sa, 0, 1, self.ga), (self.rb, rb, sb, 1, 3, self.gb)):
            far.wait_recv()

            @pl.loop(0, self.n)
            def _(m):
                sum_[m] = (got[m].astype(F32) + self.add(s, self.at(to), m)).astype(BF16)

            on.start()

    def result(self, put):
        _, _, fa, fb, ga, gb, _, _ = self.bufs
        for s, near, far, a, b in ((0, self.fa, self.ga, fa, ga), (1, self.fb, self.gb, fb, gb)):
            near.wait_recv()
            far.wait_recv()

            @pl.loop(0, self.n)
            def _(m):
                put(s, m, self.add(s, self.i, m) + (a[m].astype(F32) + b[m].astype(F32)))

    def drain(self):
        for c in (self.ra, self.rb, self.fb, self.fa, self.ga, self.gb):
            c.wait_send()


def kernel(
    g, out, gown, gsib, psend, zrel, zrec, sline, t, l1, l2, xf, xb, o, u,
    lsem, csend, crecv, rsend, rrecv, fsend, frecv, dsem,
):
    rep, x, col = lax.axis_index("rep"), lax.axis_index("row"), lax.axis_index("col")
    zh, k = lax.div(rep, 2), mod(rep, 2)
    zl, y = lax.div(col, 4), mod(col, 4)
    z = 2 * zh + zl
    q, d = psend.shape
    half = q // 2
    w = d // CHUNKS
    n8 = d // STAGES // 8
    n4 = n8 // 4

    def dev(x, y, z, k):
        return {"rep": lax.div(z, 2) * 2 + k, "row": x, "col": mod(z, 2) * 4 + y}

    sib = dev(x, y, z, 1 - k)
    zp, zm = dev(x, y, mod(z + 1, 4), k), dev(x, y, mod(z + 3, 4), k)
    yp, ym = dev(x, mod(y + 1, 4), z, k), dev(x, mod(y + 3, 4), z, k)
    xp, xm = dev(mod(x + 1, 4), y, z, k), dev(mod(x + 3, 4), y, z, k)

    def cols(c):
        return pl.ds(pl.multiple_of(c * w, w), w)

    def rows(i):
        return pl.ds(pl.multiple_of(i * q, q), q)

    def load(c):
        return pltpu.make_async_copy(g.at[:, k, :, cols(c)], gown.at[:, :, cols(c)], lsem.at[c])

    def swap(c):
        return rcopy(g.at[:, 1 - k, :, cols(c)], gsib.at[:, :, cols(c)], csend.at[0], crecv.at[0, c], sib)

    def z1(c):
        return (
            rcopy(psend.at[0:half, cols(c)], zrel.at[0, :, cols(c)], csend.at[1], crecv.at[1, c], zp),
            rcopy(psend.at[half:q, cols(c)], zrel.at[1, :, cols(c)], csend.at[2], crecv.at[2, c], zm),
        )

    def z2(c):
        return (
            rcopy(zrel.at[0, :, cols(c)], zrec.at[0, :, cols(c)], csend.at[3], crecv.at[3, c], zp),
            rcopy(zrel.at[1, :, cols(c)], zrec.at[1, :, cols(c)], csend.at[4], crecv.at[4, c], zm),
        )

    def block(j, c, part=None):
        base = (2 * mod(y + j, 4) + k) * q
        if part is None:
            return sline.at[pl.ds(pl.multiple_of(base, q), q), cols(c)]
        return sline.at[pl.ds(pl.multiple_of(base + part * half, half), half), cols(c)]

    def sblock(j, c):
        return sline.at[pl.ds(pl.multiple_of((2 * mod(y + j, 4) + 1 - k) * q, q), q), cols(c)]

    def y1(c):
        own = block(0, c)
        return (
            rcopy(own, own, csend.at[5], crecv.at[5, c], yp),
            rcopy(own, own, csend.at[6], crecv.at[6, c], ym),
        )

    def y1_landed(c):
        down, upper = block(3, c), block(1, c)
        return (
            rcopy(down, down, csend.at[5], crecv.at[5, c], yp),
            rcopy(upper, upper, csend.at[6], crecv.at[6, c], ym),
        )

    def y2(c):
        down, upper = block(3, c, 0), block(1, c, 1)
        return (
            rcopy(down, down, csend.at[7], crecv.at[7, c], yp),
            rcopy(upper, upper, csend.at[8], crecv.at[8, c], ym),
        )

    def y2_landed(c):
        lo, hi = block(2, c, 0), block(2, c, 1)
        return (
            rcopy(lo, lo, csend.at[7], crecv.at[7, c], yp),
            rcopy(hi, hi, csend.at[8], crecv.at[8, c], ym),
        )

    def share(j, c):
        blk = block(j, c)
        return rcopy(blk, blk, csend.at[9 + j], crecv.at[9 + j, c], sib)

    def share_landed(j, c):
        blk = sblock(j, c)
        return rcopy(blk, blk, csend.at[9 + j], crecv.at[9 + j, c], sib)

    @pl.loop(0, CHUNKS)
    def _(c):
        load(c).start()
        swap(c).start()

    def gather_step(step):
        c = step
        if c < CHUNKS:
            load(c).wait()
            swap(c).wait_recv()
            away = 1 - zh
            psend[:, cols(c)] = (gown[away, :, cols(c)].astype(F32) + gsib[away, :, cols(c)].astype(F32)).astype(BF16)
            for cp in z1(c):
                cp.start()
        c = step - 1
        if 0 <= c < CHUNKS:
            for cp, fwd in zip(z1(c), z2(c)):
                cp.wait_recv()
                fwd.start()
        c = step - 2
        if 0 <= c < CHUNKS:
            for cp in z2(c):
                cp.wait_recv()
            own = gown[zh, :, cols(c)].astype(F32) + gsib[zh, :, cols(c)].astype(F32)
            far = jnp.concatenate([zrec[0, :, cols(c)], zrec[1, :, cols(c)]], axis=0).astype(F32)
            sline[rows(2 * y + k), cols(c)] = (own + far).astype(BF16)
            for cp in y1(c):
                cp.start()
            share(0, c).start()
        c = step - 3
        if 0 <= c < CHUNKS:
            for cp, fwd, j in zip(y1_landed(c), y2(c), (3, 1)):
                cp.wait_recv()
                fwd.start()
                share(j, c).start()
        c = step - 4
        if 0 <= c < CHUNKS:
            for cp in y2_landed(c):
                cp.wait_recv()
            share(2, c).start()

    def first(n):
        return n * (n + 1) // 2

    strip = 2 * y + k

    def tiles(n):
        for c in range(n * PER, (n + 1) * PER):
            for j in range(4):
                share_landed(j, c).wait_recv()

        @pl.loop(0, n + 1)
        def _(m):
            lhs = sline[:, pl.ds(pl.multiple_of((8 * n + strip) * n8, n8), n8)]
            rhs = sline[:, pl.ds(pl.multiple_of(m * 8 * n8, 8 * n8), 8 * n8)]
            acc = lax.dot_general(lhs, rhs, (((0,), (0,)), ((), ())), preferred_element_type=F32)
            for j in range(8):
                t[first(n) + m, j] = acc[:, j * n8 : (j + 1) * n8].astype(BF16)

    def quarter(v):
        return pl.ds(pl.multiple_of(v * n4, n4), n4)

    def ring1(n):
        f = first(n)
        return Ring(
            x, xp, xm, n + 1,
            lambda s, p: t.at[f : f + n + 1, 2 * p + s],
            lambda s, p, m: t[f + m, 2 * p + s].astype(F32),
            [l1.at[i, f : f + n + 1] for i in range(8)],
            rsend.at[0, n], rrecv.at[0, n],
        )

    def ring2(n):
        f = first(n)
        return Ring(
            z, zp, zm, n + 1,
            lambda s, v: xb.at[s, f : f + n + 1, quarter(v), :],
            lambda s, v, m: xf[s, f + m, quarter(v), :],
            [l2.at[i, f : f + n + 1] for i in range(8)],
            rsend.at[1, n], rrecv.at[1, n],
        )

    rings1 = [ring1(n) for n in range(STAGES)]
    rings2 = [ring2(n) for n in range(STAGES)]

    def exchange(n, begin):
        f = first(n)
        rblk = 8 * n + strip

        def one(m, up, side):
            cblk = 8 * m + 2 * x
            src = o.at[f + m]
            if side == 0:
                tx, tc = lax.div(rblk, 12), lax.div(cblk, 6)
                dst = u.at[mod(rblk, 12), pl.ds(mod(cblk, 6), 2), quarter(z), :]
            else:
                tx, tc = lax.div(cblk, 12), lax.div(rblk, 6)
                dst = u.at[pl.ds(mod(cblk, 12), 2), mod(rblk, 6), quarter(z), :]
            ty, tz = mod(tc, 4), 2 * up + lax.div(tc, 4)
            mine = (tx == x) & (ty == y) & (tz == z)

            @pl.when(jnp.logical_not(mine))
            def _():
                cp = rcopy(src, dst, fsend.at[f + m, 2 * side + up], frecv.at[0], dev(tx, ty, tz, k))
                if begin:
                    cp.start()
                else:
                    cp.wait_send()

            if begin:

                @pl.when(mine)
                def _():
                    pltpu.make_async_copy(src, dst, frecv.at[0]).start()

        for up in (0, 1):

            @pl.loop(0, n + 1)
            def _(m):
                one(m, up, 0)

            if n:

                @pl.loop(0, n)
                def _(m):
                    one(m, up, 1)

    def reduce1(n):
        f = first(n)

        def put(s, m, v):
            xf[s, f + m] = v
            xb[s, f + m] = v.astype(BF16)

        rings1[n].result(put)
        rings2[n].start()

    def reduce2(n):
        f = first(n)

        def put(s, m, v):
            o[f + m, s] = v.astype(BF16)

        rings2[n].result(put)
        exchange(n, True)

    def begin(n):
        tiles(n)
        rings1[n].start()

    plan = {}

    def at(step, what, n):
        plan.setdefault(step, []).append((what, n))

    passes1 = lambda n: rings1[n].pass_on()
    passes2 = lambda n: rings2[n].pass_on()
    for n in range(STAGES):
        s0 = PER * (n + 1) + 4
        at(s0 + 1 + (n in (3, 4)), passes1, n)
        at(s0 + 4, reduce1, n)
        at(s0 + 5, passes2, n)
        at(s0 + 6, reduce2, n)
        at(s0, begin, n)
    for step in range(max(plan) + 1):
        gather_step(step)
        for what, n in plan.get(step, ()):
            what(n)

    def sent(n, ref):
        rcopy(ref, ref, csend.at[n], crecv.at[0, 0], sib).wait_send()

    sent(0, gsib)
    for n in (1, 2, 3, 4):
        sent(n, zrel.at[0])
    for n in (5, 6, 9, 10, 11, 12):
        sent(n, psend)
    for n in (7, 8):
        sent(n, zrel.at[0])

    for n in range(STAGES):
        rings1[n].drain()
        rings2[n].drain()

    whole = u.at[0:6]
    rcopy(whole, whole, dsem.at[0], frecv.at[0], sib).wait_recv()

    @pl.loop(0, 12)
    def _(i):
        for j in range(6):
            direct = lax.div(12 * x + i, 8) >= lax.div(6 * col + j, 8)
            from_me = jnp.where(direct, mod(i, 2), j % 2) == k

            @pl.when(from_me)
            def _():
                rcopy(u.at[i, j], u.at[i, j], dsem.at[0], dsem.at[1], sib).start()

    for n in range(STAGES):
        exchange(n, False)
    rcopy(whole, whole, dsem.at[0], dsem.at[1], sib).wait_recv()
    rcopy(whole, whole, dsem.at[0], dsem.at[1], sib).wait_send()
    whole_out = pltpu.make_async_copy(u, out, lsem.at[0])
    whole_out.start()
    whole_out.wait()


def gather_blocks(grad):
    _, n, d = grad.shape
    q = n // 4
    n8 = d // STAGES // 8
    n4 = n8 // 4
    count = STAGES * (STAGES + 1) // 2
    vm = pltpu.VMEM
    dma = pltpu.SemaphoreType.DMA
    return pl.pallas_call(
        kernel,
        out_shape=jax.ShapeDtypeStruct((12, 6, n8, n8), BF16),
        in_specs=[pl.BlockSpec(memory_space=pl.ANY)],
        out_specs=pl.BlockSpec(memory_space=pl.ANY),
        scratch_shapes=[
            vm((2, q, d), BF16), vm((2, q, d), BF16), vm((q, d), BF16),
            vm((2, q // 2, d), BF16), vm((2, q // 2, d), BF16),
            vm((8 * q, d), BF16), vm((count, 8, n8, n8), BF16),
            vm((8, count, n8, n8), BF16), vm((8, count, n4, n8), BF16),
            vm((2, count, n8, n8), F32), vm((2, count, n8, n8), BF16),
            vm((count, 2, n4, n8), BF16), vm((12, 6, n8, n8), BF16),
            dma((CHUNKS,)), dma((13,)), dma((13, CHUNKS)), dma((2, STAGES, 6)), dma((2, STAGES, 6)),
            dma((count, 4)), dma((1,)), dma((2,)),
        ],
        compiler_params=pltpu.CompilerParams(has_side_effects=True, vmem_limit_bytes=56 * 1024 * 1024),
    )(grad.reshape(2, 2, q, d))


GROUP = 2


def finish(blocks, statistic, gram, following):
    i0 = pl.program_id(0) * GROUP
    row0, col0 = 12 * lax.axis_index("row"), 6 * lax.axis_index("col")
    n = blocks.shape[-1]
    for i in range(GROUP):
        for j in range(6):
            direct = lax.div(row0 + i0 + i, 8) >= lax.div(col0 + j, 8)
            at = (slice(i * n, (i + 1) * n), slice(j * n, (j + 1) * n))

            @pl.when(direct)
            def _():
                gram[at] = blocks[i, j].astype(F32)

            @pl.when(jnp.logical_not(direct))
            def _():
                gram[at] = blocks[i, j].astype(F32).T

    following[...] = 0.95 * statistic[...] + 0.05 * gram[...]


def shards(grad, statistic):
    blocks = gather_blocks(grad)
    n = blocks.shape[-1]
    tile = pl.BlockSpec((GROUP * n, 6 * n), lambda i: (i, 0))
    shape = jax.ShapeDtypeStruct(statistic.shape, F32)
    return pl.pallas_call(
        finish,
        grid=(12 // GROUP,),
        out_shape=(shape, shape),
        in_specs=[pl.BlockSpec((GROUP, 6, n, n), lambda i: (i, 0, 0, 0)), tile],
        out_specs=(tile, tile),
    )(blocks, statistic)


def solution(mesh):
    return jax.shard_map(
        shards,
        mesh=mesh,
        in_specs=(P("rep", ("row", "col"), None), P("row", "col")),
        out_specs=(P("row", "col"), P("row", "col")),
        check_vma=False,
    )
```

time: 442 us -> 153 us (0.35)
  the two profiles are of different devices: /device:TPU:9 before, /device:TPU:49 now
where the time goes in v2:
time: 153 us
  Pallas kernels  152 us (99%)
    pallas_call x1, Pallas kernels, gather_blocks(): pl.pallas_call(kernel, out_shape=jax.ShapeDtypeStruct((12, 6, n8, n8), BF...  141 us
    pallas_call x1, Pallas kernels, shards(): pl.pallas_call(finish, grid=(12 // GROUP,), out_shape=(shape, shape), in_...  11.6 us

profile of v2, /device:TPU:49, one launch (start us, length us, event | category | flops | bytes accessed | tf_op | source)
XLA Modules:
  0.0 152.9 jit_solution(937753994735828192)
XLA Ops:
  0.6 140.7 %shard_map.41.blocks = bf16[12,6,128,128]{3,2,1,0:T(8,128)(2,1)} custom-call(bf16[2,2,128,6144]{3,2,1,0:T(8,128)(2,1)} %bitcast.1), custom_call_target="tpu_custom_call" | custom-call | tf_op jit(solution)/shard_map/pallas_call | solution.py:380
  141.3 11.6 %shard_map.42 = (f32[1536,768]{1,0:T(8,128)}, f32[1536,768]{1,0:T(8,128)}) custom-call(bf16[12,6,128,128]{3,2,1,0:T(8,128)(2,1)} %shard_map.41.blocks, f32[1536,768]{1,0:T(8,128)} %statistic.1), custom_call_target="tpu_custom_call" | custom-call | tf_op jit(solution)/shard_map/pallas_call | solution.py:427

commit v3 on v2

v3 whole, which is shorter than its diff:
```python
import functools

import jax
import jax.numpy as jnp
from jax import lax
from jax.experimental import pallas as pl
from jax.experimental.pallas import tpu as pltpu
from jax.sharding import PartitionSpec as P

MESH = pl.DeviceIdType.MESH
BF16 = jnp.bfloat16
F32 = jnp.float32
BLOCK = 128
STAGES = 12
WIDTHS = (1, 1, 2) + (4,) * 11
STARTS = tuple(sum(WIDTHS[:i]) for i in range(len(WIDTHS)))
CHUNKS = len(WIDTHS)
BETA_FROM = 8


def count(n):
    return n // 2 + 1


def first(n):
    return sum(count(i) for i in range(n))


TOTAL = first(STAGES)


def mod(a, n):
    return lax.rem(a, n)


def rcopy(src, dst, send, recv, device):
    return pltpu.make_async_remote_copy(
        src_ref=src, dst_ref=dst, send_sem=send, recv_sem=recv, device_id=device, device_id_type=MESH
    )


class Ring:
    def __init__(self, i, up, down, span, src, add, bufs, sends, recvs):
        lo, hi = span
        mid = lo + (hi - lo + 1) // 2
        far, near, got, total = bufs
        at = lambda j: mod(i + j, 4)
        self.i, self.add, self.bufs, self.halves = i, add, bufs, []
        for s, (a, b, long, short, j) in enumerate(((lo, mid, up, down, 3), (mid, hi, down, up, 1))):
            if a == b:
                continue
            cut = lambda ref: ref.at[a:b]
            self.halves.append((
                a, b, at(4 - j),
                rcopy(src(at(2), a, b), cut(far), sends.at[3 * s], recvs.at[3 * s], long),
                rcopy(src(at(j), a, b), cut(near), sends.at[3 * s + 1], recvs.at[3 * s + 1], short),
                rcopy(cut(total), cut(got), sends.at[3 * s + 2], recvs.at[3 * s + 2], long),
            ))

    def start(self):
        for h in self.halves:
            h[3].start()
        for h in self.halves:
            h[4].start()

    def pass_on(self):
        far, _, _, total = self.bufs
        for a, b, to, one, _, on in self.halves:
            one.wait_recv()

            @pl.loop(a, b)
            def _(m):
                total[m] = (far[m].astype(F32) + self.add(to, m)).astype(BF16)

            on.start()

    def result(self, put):
        _, near, got, _ = self.bufs
        for a, b, _, _, two, on in self.halves:
            two.wait_recv()
            on.wait_recv()

            @pl.loop(a, b)
            def _(m):
                put(m, self.add(self.i, m) + (near[m].astype(F32) + got[m].astype(F32)))

    def drain(self):
        for h in self.halves:
            for c in h[3:]:
                c.wait_send()


def kernel(
    g, out, gown, gsib, psend, zrel, zrec, sline, own, t, l1, l2, xf, xb, o, u,
    lsem, csend, crecv, rsend, rrecv, fsend, frecv, dsem,
):
    rep, x, col = lax.axis_index("rep"), lax.axis_index("row"), lax.axis_index("col")
    zh, k = lax.div(rep, 2), mod(rep, 2)
    zl, y = lax.div(col, 4), mod(col, 4)
    z = 2 * zh + zl
    q, d = psend.shape
    half = q // 2
    bs = BLOCK
    b4 = bs // 4

    def dev(x, y, z, k):
        return {"rep": lax.div(z, 2) * 2 + k, "row": x, "col": mod(z, 2) * 4 + y}

    sib = dev(x, y, z, 1 - k)
    zp, zm = dev(x, y, mod(z + 1, 4), k), dev(x, y, mod(z + 3, 4), k)
    yp, ym = dev(x, mod(y + 1, 4), z, k), dev(x, mod(y + 3, 4), z, k)
    xp, xm = dev(mod(x + 1, 4), y, z, k), dev(mod(x + 3, 4), y, z, k)

    def cols(c):
        return slice(STARTS[c] * bs, (STARTS[c] + WIDTHS[c]) * bs)

    def rows(i):
        return pl.ds(pl.multiple_of(i * q, q), q)

    def load(c):
        return pltpu.make_async_copy(g.at[:, k, :, cols(c)], gown.at[:, :, cols(c)], lsem.at[c])

    def swap(c):
        return rcopy(g.at[:, 1 - k, :, cols(c)], gsib.at[:, :, cols(c)], csend.at[0], crecv.at[0, c], sib)

    def z1(c):
        return (
            rcopy(psend.at[0:half, cols(c)], zrel.at[0, :, cols(c)], csend.at[1], crecv.at[1, c], zp),
            rcopy(psend.at[half:q, cols(c)], zrel.at[1, :, cols(c)], csend.at[2], crecv.at[2, c], zm),
        )

    def z2(c):
        return (
            rcopy(zrel.at[0, :, cols(c)], zrec.at[0, :, cols(c)], csend.at[3], crecv.at[3, c], zp),
            rcopy(zrel.at[1, :, cols(c)], zrec.at[1, :, cols(c)], csend.at[4], crecv.at[4, c], zm),
        )

    def block(j, c, part=None):
        base = (2 * mod(y + j, 4) + k) * q
        if part is None:
            return sline.at[pl.ds(pl.multiple_of(base, q), q), cols(c)]
        return sline.at[pl.ds(pl.multiple_of(base + part * half, half), half), cols(c)]

    def sblock(j, c):
        return sline.at[pl.ds(pl.multiple_of((2 * mod(y + j, 4) + 1 - k) * q, q), q), cols(c)]

    def y1(c):
        own = block(0, c)
        return (
            rcopy(own, own, csend.at[5], crecv.at[5, c], yp),
            rcopy(own, own, csend.at[6], crecv.at[6, c], ym),
        )

    def y1_landed(c):
        down, upper = block(3, c), block(1, c)
        return (
            rcopy(down, down, csend.at[5], crecv.at[5, c], yp),
            rcopy(upper, upper, csend.at[6], crecv.at[6, c], ym),
        )

    def y2(c):
        down, upper = block(3, c, 0), block(1, c, 1)
        return (
            rcopy(down, down, csend.at[7], crecv.at[7, c], yp),
            rcopy(upper, upper, csend.at[8], crecv.at[8, c], ym),
        )

    def y2_landed(c):
        lo, hi = block(2, c, 0), block(2, c, 1)
        return (
            rcopy(lo, lo, csend.at[7], crecv.at[7, c], yp),
            rcopy(hi, hi, csend.at[8], crecv.at[8, c], ym),
        )

    def share(j, c):
        blk = block(j, c)
        return rcopy(blk, blk, csend.at[9 + j], crecv.at[9 + j, c], sib)

    def share_landed(j, c):
        blk = sblock(j, c)
        return rcopy(blk, blk, csend.at[9 + j], crecv.at[9 + j, c], sib)

    for c in range(CHUNKS):
        load(c).start()
        swap(c).start()
    own[...] = jnp.zeros_like(own)

    def gather_step(step):
        c = step
        if c < CHUNKS:
            load(c).wait()
            swap(c).wait_recv()
            away = 1 - zh
            psend[:, cols(c)] = (gown[away, :, cols(c)].astype(F32) + gsib[away, :, cols(c)].astype(F32)).astype(BF16)
            for cp in z1(c):
                cp.start()
        c = step - 1
        if 0 <= c < CHUNKS:
            for cp, fwd in zip(z1(c), z2(c)):
                cp.wait_recv()
                fwd.start()
        c = step - 2
        if 0 <= c < CHUNKS:
            for cp in z2(c):
                cp.wait_recv()
            own = gown[zh, :, cols(c)].astype(F32) + gsib[zh, :, cols(c)].astype(F32)
            far = jnp.concatenate([zrec[0, :, cols(c)], zrec[1, :, cols(c)]], axis=0).astype(F32)
            sline[rows(2 * y + k), cols(c)] = (own + far).astype(BF16)
            for cp in y1(c):
                cp.start()
            share(0, c).start()
        c = step - 3
        if 0 <= c < CHUNKS:
            for cp, fwd, j in zip(y1_landed(c), y2(c), (3, 1)):
                cp.wait_recv()
                fwd.start()
                share(j, c).start()
        c = step - 4
        if 0 <= c < CHUNKS:
            for cp in y2_landed(c):
                cp.wait_recv()
            share(2, c).start()

    strip = 2 * y + k

    def tiles(n):
        for c in range(CHUNKS):
            if STARTS[c] // 4 == n:
                for j in range(4):
                    share_landed(j, c).wait_recv()
        last = n // 2

        @pl.when((strip >= 4) if n % 2 else (strip < 4))
        def _():
            mine = pl.ds(pl.multiple_of((8 * last + strip) * bs, bs), bs)
            own[:, last * bs : (last + 1) * bs] = sline[:, mine]

        lhs = sline[:, 4 * n * bs : 4 * (n + 1) * bs]
        acc = lax.dot_general(
            lhs, own[:, : count(n) * bs], (((0,), (0,)), ((), ())), preferred_element_type=F32
        )
        for m in range(count(n)):
            for p in range(4):
                t[first(n) + m, p] = acc[p * bs : (p + 1) * bs, m * bs : (m + 1) * bs].astype(BF16)

    def quarter(v):
        return pl.ds(pl.multiple_of(v * b4, b4), b4)

    parts = []
    for n in range(STAGES):
        a, b = first(n), first(n + 1)
        h = b if n < BETA_FROM else a + (b - a + 1) // 2
        parts.append([(a, h, True)] + ([(h, b, False)] if h < b else []))
    rings1, rings2, used = [], [], 0
    for n in range(STAGES):
        ones, twos = [], []
        for a, b, x_first in parts[n]:
            along = ((x, xp, xm), (z, zp, zm))
            one, two = along if x_first else along[::-1]
            ones.append(Ring(
                *one, (a, b),
                lambda p, a, b: t.at[a:b, p],
                lambda p, m: t[m, p].astype(F32),
                [l1.at[i] for i in range(4)],
                rsend.at[0, used], rrecv.at[0, used],
            ))
            twos.append(Ring(
                *two, (a, b),
                lambda v, a, b: xb.at[a:b, quarter(v), :],
                lambda v, m: xf[m, quarter(v), :],
                [l2.at[i] for i in range(4)],
                rsend.at[1, used], rrecv.at[1, used],
            ))
            used += 1
        rings1.append(ones)
        rings2.append(twos)

    def exchange(n, begin):
        for a, b, x_first in parts[n]:
            p1, p2 = (x, z) if x_first else (z, x)
            rblk = 4 * n + p1

            def one(f, up, side):
                m = f - first(n)
                cblk = 8 * m + strip
                stage = lax.div(cblk, 4)
                wanted = (stage <= n) if side == 0 else (stage < n)
                rr, cc = (rblk, cblk) if side == 0 else (cblk, rblk)
                tx, tc = lax.div(rr, 12), lax.div(cc, 6)
                src = o.at[f]
                dst = u.at[mod(rr, 12), mod(cc, 6), quarter(p2), :]
                ty, tz = mod(tc, 4), 2 * up + lax.div(tc, 4)
                mine = (tx == x) & (ty == y) & (tz == z)

                @pl.when(wanted & jnp.logical_not(mine))
                def _():
                    cp = rcopy(src, dst, fsend.at[f, 2 * side + up], frecv.at[0], dev(tx, ty, tz, k))
                    if begin:
                        cp.start()
                    else:
                        cp.wait_send()

                if begin:

                    @pl.when(wanted & mine)
                    def _():
                        pltpu.make_async_copy(src, dst, frecv.at[0]).start()

            @pl.loop(a, b)
            def _(f):
                for side in (0, 1):
                    for up in (0, 1):
                        one(f, up, side)

    def begin(n):
        tiles(n)
        for r in rings1[n]:
            r.start()

    def pass1(n):
        for r in rings1[n]:
            r.pass_on()

    def reduce1(n):
        def put(m, v):
            xf[m] = v
            xb[m] = v.astype(BF16)

        for r, r2 in zip(rings1[n], rings2[n]):
            r.result(put)
            r2.start()

    def pass2(n):
        for r in rings2[n]:
            r.pass_on()

    def reduce2(n):
        def put(m, v):
            o[m] = v.astype(BF16)

        for r in rings2[n]:
            r.result(put)
        exchange(n, True)

    plan = {}
    for n in range(STAGES):
        step = n + 7
        for after, what in ((0, begin), (1 if n < 7 else 2, pass1), (2, reduce1), (1, pass2), (1, reduce2)):
            step += after
            plan.setdefault(step, []).append((what, n))
    for step in range(max(plan) + 1):
        gather_step(step)
        for what, n in plan.get(step, ()):
            what(n)

    def sent(n, ref):
        rcopy(ref, ref, csend.at[n], crecv.at[0, 0], sib).wait_send()

    sent(0, gsib)
    for n in (1, 2, 3, 4):
        sent(n, zrel.at[0])
    for n in (5, 6, 9, 10, 11, 12):
        sent(n, psend)
    for n in (7, 8):
        sent(n, zrel.at[0])

    for n in range(STAGES):
        for r in rings1[n] + rings2[n]:
            r.drain()

    whole = u.at[0:6]
    rcopy(whole, whole, dsem.at[0], frecv.at[0], sib).wait_recv()

    @pl.loop(0, 12)
    def _(i):
        for j in range(6):
            direct = lax.div(12 * x + i, 4) >= lax.div(6 * col + j, 4)
            from_me = jnp.where(direct, j % 2, mod(i, 2)) == k

            @pl.when(from_me)
            def _():
                rcopy(u.at[i, j], u.at[i, j], dsem.at[0], dsem.at[1], sib).start()

    for n in range(STAGES):
        exchange(n, False)
    rcopy(whole, whole, dsem.at[0], dsem.at[1], sib).wait_recv()
    rcopy(whole, whole, dsem.at[0], dsem.at[1], sib).wait_send()
    whole_out = pltpu.make_async_copy(u, out, lsem.at[0])
    whole_out.start()
    whole_out.wait()


def gather_blocks(grad):
    _, n, d = grad.shape
    q, bs = n // 4, BLOCK
    b4 = bs // 4
    subs = STAGES + STAGES - BETA_FROM
    vm = pltpu.VMEM
    dma = pltpu.SemaphoreType.DMA
    return pl.pallas_call(
        kernel,
        out_shape=jax.ShapeDtypeStruct((12, 6, bs, bs), BF16),
        in_specs=[pl.BlockSpec(memory_space=pl.ANY)],
        out_specs=pl.BlockSpec(memory_space=pl.ANY),
        scratch_shapes=[
            vm((2, q, d), BF16), vm((2, q, d), BF16), vm((q, d), BF16),
            vm((2, q // 2, d), BF16), vm((2, q // 2, d), BF16),
            vm((8 * q, d), BF16), vm((8 * q, d // 8), BF16), vm((TOTAL, 4, bs, bs), BF16),
            vm((4, TOTAL, bs, bs), BF16), vm((4, TOTAL, b4, bs), BF16),
            vm((TOTAL, bs, bs), F32), vm((TOTAL, bs, bs), BF16),
            vm((TOTAL, b4, bs), BF16), vm((12, 6, bs, bs), BF16),
            dma((CHUNKS,)), dma((13,)), dma((13, CHUNKS)), dma((2, subs, 6)), dma((2, subs, 6)),
            dma((TOTAL, 4)), dma((1,)), dma((2,)),
        ],
        compiler_params=pltpu.CompilerParams(has_side_effects=True, vmem_limit_bytes=56 * 1024 * 1024),
    )(grad.reshape(2, 2, q, d))


GROUP = 2


def finish(blocks, statistic, gram, following):
    i0 = pl.program_id(0) * GROUP
    row0, col0 = 12 * lax.axis_index("row"), 6 * lax.axis_index("col")
    n = blocks.shape[-1]
    for i in range(GROUP):
        for j in range(6):
            direct = lax.div(row0 + i0 + i, 4) >= lax.div(col0 + j, 4)
            at = (slice(i * n, (i + 1) * n), slice(j * n, (j + 1) * n))

            @pl.when(direct)
            def _():
                gram[at] = blocks[i, j].astype(F32)

            @pl.when(jnp.logical_not(direct))
            def _():
                gram[at] = blocks[i, j].astype(F32).T

    following[...] = 0.95 * statistic[...] + 0.05 * gram[...]


def shards(grad, statistic):
    blocks = gather_blocks(grad)
    n = blocks.shape[-1]
    tile = pl.BlockSpec((GROUP * n, 6 * n), lambda i: (i, 0))
    shape = jax.ShapeDtypeStruct(statistic.shape, F32)
    return pl.pallas_call(
        finish,
        grid=(12 // GROUP,),
        out_shape=(shape, shape),
        in_specs=[pl.BlockSpec((GROUP, 6, n, n), lambda i: (i, 0, 0, 0)), tile],
        out_specs=(tile, tile),
    )(blocks, statistic)


def solution(mesh):
    return jax.shard_map(
        shards,
        mesh=mesh,
        in_specs=(P("rep", ("row", "col"), None), P("row", "col")),
        out_specs=(P("row", "col"), P("row", "col")),
        check_vma=False,
    )
```

time: 153 us -> 164 us (1.072)
  the two profiles are of different devices: /device:TPU:49 before, /device:TPU:121 now
where the time goes in v3:
time: 164 us
  Pallas kernels  163 us (99%)
    pallas_call x1, Pallas kernels, gather_blocks(): pl.pallas_call(kernel, out_shape=jax.ShapeDtypeStruct((12, 6, bs, bs), BF...  152 us
    pallas_call x1, Pallas kernels, shards(): pl.pallas_call(finish, grid=(12 // GROUP,), out_shape=(shape, shape), in_...  11.6 us

profile of v3, /device:TPU:121, one launch (start us, length us, event | category | flops | bytes accessed | tf_op | source)
XLA Modules:
  0.0 164.1 jit_solution(8268361718429895112)
XLA Ops:
  0.6 151.9 %shard_map.41.blocks = bf16[12,6,128,128]{3,2,1,0:T(8,128)(2,1)} custom-call(bf16[2,2,128,6144]{3,2,1,0:T(8,128)(2,1)} %bitcast.1), custom_call_target="tpu_custom_call" | custom-call | tf_op jit(solution)/shard_map/pallas_call | solution.py:400
  152.5 11.6 %shard_map.42 = (f32[1536,768]{1,0:T(8,128)}, f32[1536,768]{1,0:T(8,128)}) custom-call(bf16[12,6,128,128]{3,2,1,0:T(8,128)(2,1)} %shard_map.41.blocks, f32[1536,768]{1,0:T(8,128)} %statistic.1), custom_call_target="tpu_custom_call" | custom-call | tf_op jit(solution)/shard_map/pallas_call | solution.py:447

commit v4 on v3

--- a/solution.py
+++ b/solution.py
@@ -12,7 +12,7 @@
 F32 = jnp.float32
 BLOCK = 128
 STAGES = 12
-WIDTHS = (1, 1, 2) + (4,) * 11
+WIDTHS = (4,) * 12
 STARTS = tuple(sum(WIDTHS[:i]) for i in range(len(WIDTHS)))
 CHUNKS = len(WIDTHS)
 BETA_FROM = 8
@@ -117,11 +117,22 @@
     def rows(i):
         return pl.ds(pl.multiple_of(i * q, q), q)
 
+    def strided(c):
+        return [(pl.ds((c + STAGES * i) * bs, bs), pl.ds((4 * c + i) * bs, bs)) for i in range(4)]
+
     def load(c):
-        return pltpu.make_async_copy(g.at[:, k, :, cols(c)], gown.at[:, :, cols(c)], lsem.at[c])
+        for there, here in strided(c):
+            pltpu.make_async_copy(g.at[:, k, :, there], gown.at[:, :, here], lsem.at[c]).start()
 
     def swap(c):
-        return rcopy(g.at[:, 1 - k, :, cols(c)], gsib.at[:, :, cols(c)], csend.at[0], crecv.at[0, c], sib)
+        for there, here in strided(c):
+            rcopy(g.at[:, 1 - k, :, there], gsib.at[:, :, here], csend.at[0], crecv.at[0, c], sib).start()
+
+    def loaded(c):
+        whole = gown.at[:, :, cols(c)]
+        pltpu.make_async_copy(whole, whole, lsem.at[c]).wait()
+        whole = gsib.at[:, :, cols(c)]
+        rcopy(whole, whole, csend.at[0], crecv.at[0, c], sib).wait_recv()
 
     def z1(c):
         return (
@@ -181,15 +192,14 @@
         return rcopy(blk, blk, csend.at[9 + j], crecv.at[9 + j, c], sib)
 
     for c in range(CHUNKS):
-        load(c).start()
-        swap(c).start()
+        load(c)
+        swap(c)
     own[...] = jnp.zeros_like(own)
 
     def gather_step(step):
         c = step
         if c < CHUNKS:
-            load(c).wait()
-            swap(c).wait_recv()
+            loaded(c)
             away = 1 - zh
             psend[:, cols(c)] = (gown[away, :, cols(c)].astype(F32) + gsib[away, :, cols(c)].astype(F32)).astype(BF16)
             for cp in z1(c):
@@ -221,7 +231,8 @@
                 cp.wait_recv()
             share(2, c).start()
 
-    strip = 2 * y + k
+    turn = 2 * mod(y, 2) + lax.div(y, 2)
+    strip = 4 * k + turn
 
     def tiles(n):
         for c in range(CHUNKS):
@@ -230,7 +241,7 @@
                     share_landed(j, c).wait_recv()
         last = n // 2
 
-        @pl.when((strip >= 4) if n % 2 else (strip < 4))
+        @pl.when(k == n % 2)
         def _():
             mine = pl.ds(pl.multiple_of((8 * last + strip) * bs, bs), bs)
             own[:, last * bs : (last + 1) * bs] = sline[:, mine]
@@ -278,12 +289,12 @@
     def exchange(n, begin):
         for a, b, x_first in parts[n]:
             p1, p2 = (x, z) if x_first else (z, x)
-            rblk = 4 * n + p1
+            rblk = n + STAGES * p1
 
             def one(f, up, side):
                 m = f - first(n)
-                cblk = 8 * m + strip
-                stage = lax.div(cblk, 4)
+                stage = 2 * m + k
+                cblk = stage + STAGES * turn
                 wanted = (stage <= n) if side == 0 else (stage < n)
                 rr, cc = (rblk, cblk) if side == 0 else (cblk, rblk)
                 tx, tc = lax.div(rr, 12), lax.div(cc, 6)
@@ -344,7 +355,7 @@
 
     plan = {}
     for n in range(STAGES):
-        step = n + 7
+        step = n + 5
         for after, what in ((0, begin), (1 if n < 7 else 2, pass1), (2, reduce1), (1, pass2), (1, reduce2)):
             step += after
             plan.setdefault(step, []).append((what, n))
@@ -368,13 +379,17 @@
         for r in rings1[n] + rings2[n]:
             r.drain()
 
-    whole = u.at[0:6]
-    rcopy(whole, whole, dsem.at[0], frecv.at[0], sib).wait_recv()
+    sized = (l1.at[0, 0:39], l1.at[0, 0:33])
+    for core in (0, 1):
+
+        @pl.when(k == core)
+        def _():
+            rcopy(sized[core], sized[core], dsem.at[0], frecv.at[0], sib).wait_recv()
 
     @pl.loop(0, 12)
     def _(i):
         for j in range(6):
-            direct = lax.div(12 * x + i, 4) >= lax.div(6 * col + j, 4)
+            direct = i >= 6 * mod(col, 2) + j
             from_me = jnp.where(direct, j % 2, mod(i, 2)) == k
 
             @pl.when(from_me)
@@ -383,8 +398,13 @@
 
     for n in range(STAGES):
         exchange(n, False)
-    rcopy(whole, whole, dsem.at[0], dsem.at[1], sib).wait_recv()
-    rcopy(whole, whole, dsem.at[0], dsem.at[1], sib).wait_send()
+    for core in (0, 1):
+
+        @pl.when(k == core)
+        def _():
+            rcopy(sized[1 - core], sized[1 - core], dsem.at[0], dsem.at[1], sib).wait_recv()
+            rcopy(sized[core], sized[core], dsem.at[0], dsem.at[1], sib).wait_send()
+
     whole_out = pltpu.make_async_copy(u, out, lsem.at[0])
     whole_out.start()
     whole_out.wait()
@@ -421,11 +441,11 @@
 
 def finish(blocks, statistic, gram, following):
     i0 = pl.program_id(0) * GROUP
-    row0, col0 = 12 * lax.axis_index("row"), 6 * lax.axis_index("col")
+    col0 = 6 * mod(lax.axis_index("col"), 2)
     n = blocks.shape[-1]
     for i in range(GROUP):
         for j in range(6):
-            direct = lax.div(row0 + i0 + i, 4) >= lax.div(col0 + j, 4)
+            direct = i0 + i >= col0 + j
             at = (slice(i * n, (i + 1) * n), slice(j * n, (j + 1) * n))
 
             @pl.when(direct)

time: 164 us -> 154 us (0.939)
  the two profiles are of different devices: /device:TPU:121 before, /device:TPU:9 now
where the time goes in v4:
time: 154 us; the launch traced here: 153 us
  Pallas kernels  153 us (99%)
    pallas_call x1, Pallas kernels, gather_blocks(): pl.pallas_call(kernel, out_shape=jax.ShapeDtypeStruct((12, 6, bs, bs), BF...  142 us
    pallas_call x1, Pallas kernels, shards(): pl.pallas_call(finish, grid=(12 // GROUP,), out_shape=(shape, shape), in_...  10.3 us

profile of v4, /device:TPU:9, one launch (start us, length us, event | category | flops | bytes accessed | tf_op | source)
XLA Modules:
  0.0 153.4 jit_solution(7921998421950636098)
XLA Ops:
  0.6 142.4 %shard_map.41.blocks = bf16[12,6,128,128]{3,2,1,0:T(8,128)(2,1)} custom-call(bf16[2,2,128,6144]{3,2,1,0:T(8,128)(2,1)} %bitcast.1), custom_call_target="tpu_custom_call" | custom-call | tf_op jit(solution)/shard_map/pallas_call | solution.py:420
  143.0 10.3 %shard_map.42 = (f32[1536,768]{1,0:T(8,128)}, f32[1536,768]{1,0:T(8,128)}) custom-call(bf16[12,6,128,128]{3,2,1,0:T(8,128)(2,1)} %shard_map.41.blocks, f32[1536,768]{1,0:T(8,128)} %statistic.1), custom_call_target="tpu_custom_call" | custom-call | tf_op jit(solution)/shard_map/pallas_call | solution.py:467

commit v5 on v4

--- a/solution.py
+++ b/solution.py
@@ -40,21 +40,22 @@
 
 
 class Ring:
-    def __init__(self, i, up, down, span, src, add, bufs, sends, recvs):
+    def __init__(self, i, up, down, span, src, add, bufs, pair, sends, recvs):
         lo, hi = span
         mid = lo + (hi - lo + 1) // 2
         far, near, got, total = bufs
         at = lambda j: mod(i + j, 4)
         self.i, self.add, self.bufs, self.halves = i, add, bufs, []
+        self.span, self.last, self.pair, self.up = span, recvs.at[2], pair, up
         for s, (a, b, long, short, j) in enumerate(((lo, mid, up, down, 3), (mid, hi, down, up, 1))):
             if a == b:
                 continue
             cut = lambda ref: ref.at[a:b]
             self.halves.append((
                 a, b, at(4 - j),
-                rcopy(src(at(2), a, b), cut(far), sends.at[3 * s], recvs.at[3 * s], long),
-                rcopy(src(at(j), a, b), cut(near), sends.at[3 * s + 1], recvs.at[3 * s + 1], short),
-                rcopy(cut(total), cut(got), sends.at[3 * s + 2], recvs.at[3 * s + 2], long),
+                rcopy(src(at(2), a, b), cut(far), sends.at[s], recvs.at[s], long),
+                rcopy(src(at(j), a, b), cut(near), sends.at[s], recvs.at[2], short),
+                rcopy(cut(total), cut(got), sends.at[s], recvs.at[2], long),
             ))
 
     def start(self):
@@ -76,23 +77,18 @@
 
     def result(self, put):
         _, near, got, _ = self.bufs
-        for a, b, _, _, two, on in self.halves:
-            two.wait_recv()
-            on.wait_recv()
+        both = self.pair.at[:, self.span[0] : self.span[1]]
+        rcopy(both, both, self.last, self.last, self.up).wait_recv()
+        for a, b, *_ in self.halves:
 
             @pl.loop(a, b)
             def _(m):
                 put(m, self.add(self.i, m) + (near[m].astype(F32) + got[m].astype(F32)))
 
-    def drain(self):
-        for h in self.halves:
-            for c in h[3:]:
-                c.wait_send()
-
 
 def kernel(
-    g, out, gown, gsib, psend, zrel, zrec, sline, own, t, l1, l2, xf, xb, o, u,
-    lsem, csend, crecv, rsend, rrecv, fsend, frecv, dsem,
+    g, out, gown, gsib, psend, zrel, zrec, sline, own, t, l1, l2, xf, xb, o, u, spare,
+    lsem, csend, crecv, rsend, rrecv, fsem, dsem,
 ):
     rep, x, col = lax.axis_index("rep"), lax.axis_index("row"), lax.axis_index("col")
     zh, k = lax.div(rep, 2), mod(rep, 2)
@@ -152,9 +148,6 @@
             return sline.at[pl.ds(pl.multiple_of(base, q), q), cols(c)]
         return sline.at[pl.ds(pl.multiple_of(base + part * half, half), half), cols(c)]
 
-    def sblock(j, c):
-        return sline.at[pl.ds(pl.multiple_of((2 * mod(y + j, 4) + 1 - k) * q, q), q), cols(c)]
-
     def y1(c):
         own = block(0, c)
         return (
@@ -185,11 +178,11 @@
 
     def share(j, c):
         blk = block(j, c)
-        return rcopy(blk, blk, csend.at[9 + j], crecv.at[9 + j, c], sib)
-
-    def share_landed(j, c):
-        blk = sblock(j, c)
-        return rcopy(blk, blk, csend.at[9 + j], crecv.at[9 + j, c], sib)
+        return rcopy(blk, blk, csend.at[9], crecv.at[9, c], sib)
+
+    def shares_landed(c):
+        four = sline.at[0 : 4 * q, cols(c)]
+        rcopy(four, four, csend.at[9], crecv.at[9, c], sib).wait_recv()
 
     for c in range(CHUNKS):
         load(c)
@@ -237,8 +230,7 @@
     def tiles(n):
         for c in range(CHUNKS):
             if STARTS[c] // 4 == n:
-                for j in range(4):
-                    share_landed(j, c).wait_recv()
+                shares_landed(c)
         last = n // 2
 
         @pl.when(k == n % 2)
@@ -273,20 +265,22 @@
                 lambda p, a, b: t.at[a:b, p],
                 lambda p, m: t[m, p].astype(F32),
                 [l1.at[i] for i in range(4)],
-                rsend.at[0, used], rrecv.at[0, used],
+                l1.at[0:2],
+                rsend.at[0], rrecv.at[0, used],
             ))
             twos.append(Ring(
                 *two, (a, b),
                 lambda v, a, b: xb.at[a:b, quarter(v), :],
                 lambda v, m: xf[m, quarter(v), :],
                 [l2.at[i] for i in range(4)],
-                rsend.at[1, used], rrecv.at[1, used],
+                l2.at[0:2],
+                rsend.at[1], rrecv.at[1, used],
             ))
             used += 1
         rings1.append(ones)
         rings2.append(twos)
 
-    def exchange(n, begin):
+    def exchange(n):
         for a, b, x_first in parts[n]:
             p1, p2 = (x, z) if x_first else (z, x)
             rblk = n + STAGES * p1
@@ -305,17 +299,12 @@
 
                 @pl.when(wanted & jnp.logical_not(mine))
                 def _():
-                    cp = rcopy(src, dst, fsend.at[f, 2 * side + up], frecv.at[0], dev(tx, ty, tz, k))
-                    if begin:
-                        cp.start()
-                    else:
-                        cp.wait_send()
-
-                if begin:
-
-                    @pl.when(wanted & mine)
-                    def _():
-                        pltpu.make_async_copy(src, dst, frecv.at[0]).start()
+                    rcopy(src, dst, fsem.at[0], fsem.at[1], dev(tx, ty, tz, k)).start()
+
+                @pl.when(wanted & mine)
+                def _():
+                    pltpu.make_async_copy(src, dst, fsem.at[1]).start()
+                    pltpu.make_async_copy(src, spare.at[f, 2 * side + up], fsem.at[0]).start()
 
             @pl.loop(a, b)
             def _(f):
@@ -351,18 +340,21 @@
 
         for r in rings2[n]:
             r.result(put)
-        exchange(n, True)
-
-    plan = {}
+        exchange(n)
+
+    plan = []
     for n in range(STAGES):
-        step = n + 5
-        for after, what in ((0, begin), (1 if n < 7 else 2, pass1), (2, reduce1), (1, pass2), (1, reduce2)):
-            step += after
-            plan.setdefault(step, []).append((what, n))
-    for step in range(max(plan) + 1):
+        for after, what in ((0, begin), (1, pass1), (2.3, reduce1), (3.1, pass2), (3.9, reduce2)):
+            plan.append((n + 5 + after, n, what))
+    plan.sort(key=lambda item: item[:2])
+    steps = CHUNKS + 4
+    for step in range(steps):
         gather_step(step)
-        for what, n in plan.get(step, ()):
+        while plan and plan[0][0] <= step:
+            _, n, what = plan.pop(0)
             what(n)
+    for _, n, what in plan:
+        what(n)
 
     def sent(n, ref):
         rcopy(ref, ref, csend.at[n], crecv.at[0, 0], sib).wait_send()
@@ -370,21 +362,25 @@
     sent(0, gsib)
     for n in (1, 2, 3, 4):
         sent(n, zrel.at[0])
-    for n in (5, 6, 9, 10, 11, 12):
+    for n in (5, 6):
         sent(n, psend)
+    sent(9, sline.at[0 : 4 * q])
     for n in (7, 8):
         sent(n, zrel.at[0])
 
-    for n in range(STAGES):
-        for r in rings1[n] + rings2[n]:
-            r.drain()
+    ups = sum((hi - lo + 1) // 2 for ps in parts for lo, hi, _ in ps)
+    for level, ref in ((0, l1), (1, l2)):
+        for half_, blocks in ((0, ups), (1, TOTAL - ups)):
+            done = ref.at[0:3, 0:blocks]
+            rcopy(done, done, rsend.at[level, half_], rrecv.at[0, 0, 0], sib).wait_send()
 
     sized = (l1.at[0, 0:39], l1.at[0, 0:33])
     for core in (0, 1):
 
         @pl.when(k == core)
         def _():
-            rcopy(sized[core], sized[core], dsem.at[0], frecv.at[0], sib).wait_recv()
+            rcopy(sized[core], sized[core], fsem.at[0], fsem.at[1], sib).wait_recv()
+            rcopy(sized[core], sized[core], fsem.at[0], fsem.at[1], sib).wait_send()
 
     @pl.loop(0, 12)
     def _(i):
@@ -396,8 +392,6 @@
             def _():
                 rcopy(u.at[i, j], u.at[i, j], dsem.at[0], dsem.at[1], sib).start()
 
-    for n in range(STAGES):
-        exchange(n, False)
     for core in (0, 1):
 
         @pl.when(k == core)
@@ -428,48 +422,67 @@
             vm((8 * q, d), BF16), vm((8 * q, d // 8), BF16), vm((TOTAL, 4, bs, bs), BF16),
             vm((4, TOTAL, bs, bs), BF16), vm((4, TOTAL, b4, bs), BF16),
             vm((TOTAL, bs, bs), F32), vm((TOTAL, bs, bs), BF16),
-            vm((TOTAL, b4, bs), BF16), vm((12, 6, bs, bs), BF16),
-            dma((CHUNKS,)), dma((13,)), dma((13, CHUNKS)), dma((2, subs, 6)), dma((2, subs, 6)),
-            dma((TOTAL, 4)), dma((1,)), dma((2,)),
+            vm((TOTAL, b4, bs), BF16), vm((12, 6, bs, bs), BF16), vm((TOTAL, 4, b4, bs), BF16),
+            dma((CHUNKS,)), dma((10,)), dma((10, CHUNKS)), dma((2, 2)), dma((2, subs, 3)), dma((2,)), dma((2,)),
         ],
         compiler_params=pltpu.CompilerParams(has_side_effects=True, vmem_limit_bytes=56 * 1024 * 1024),
     )(grad.reshape(2, 2, q, d))
 
 
-GROUP = 2
-
-
-def finish(blocks, statistic, gram, following):
-    i0 = pl.program_id(0) * GROUP
+def finish(blocks, statistic, gram, following, ub, st, gr, fo, insem, outsem):
+    n = ub.shape[-1]
     col0 = 6 * mod(lax.axis_index("col"), 2)
-    n = blocks.shape[-1]
-    for i in range(GROUP):
+
+    def band(i):
+        return pl.ds(pl.multiple_of(i * n, n), n)
+
+    def reads(i):
+        return (
+            pltpu.make_async_copy(blocks.at[i], ub.at[i], insem.at[0, i]),
+            pltpu.make_async_copy(statistic.at[band(i), :], st.at[band(i), :], insem.at[1, i]),
+        )
+
+    @pl.loop(0, 12)
+    def _(i):
+        for cp in reads(i):
+            cp.start()
+
+    @pl.loop(0, 12)
+    def _(i):
+        for cp in reads(i):
+            cp.wait()
         for j in range(6):
-            direct = i0 + i >= col0 + j
-            at = (slice(i * n, (i + 1) * n), slice(j * n, (j + 1) * n))
-
-            @pl.when(direct)
+            at = (band(i), slice(j * n, (j + 1) * n))
+
+            @pl.when(i >= col0 + j)
             def _():
-                gram[at] = blocks[i, j].astype(F32)
-
-            @pl.when(jnp.logical_not(direct))
+                gr[at] = ub[i, j].astype(F32)
+
+            @pl.when(i < col0 + j)
             def _():
-                gram[at] = blocks[i, j].astype(F32).T
-
-    following[...] = 0.95 * statistic[...] + 0.05 * gram[...]
+                gr[at] = ub[i, j].astype(F32).T
+
+        rows = (band(i), slice(None))
+        fo[rows] = 0.95 * st[rows] + 0.05 * gr[rows]
+        pltpu.make_async_copy(gr.at[rows], gram.at[rows], outsem.at[0]).start()
+        pltpu.make_async_copy(fo.at[rows], following.at[rows], outsem.at[1]).start()
+
+    pltpu.make_async_copy(gr, gram, outsem.at[0]).wait()
+    pltpu.make_async_copy(fo, following, outsem.at[1]).wait()
 
 
 def shards(grad, statistic):
     blocks = gather_blocks(grad)
-    n = blocks.shape[-1]
-    tile = pl.BlockSpec((GROUP * n, 6 * n), lambda i: (i, 0))
     shape = jax.ShapeDtypeStruct(statistic.shape, F32)
+    whole = pltpu.VMEM(statistic.shape, F32)
+    dma = pltpu.SemaphoreType.DMA
     return pl.pallas_call(
         finish,
-        grid=(12 // GROUP,),
         out_shape=(shape, shape),
-        in_specs=[pl.BlockSpec((GROUP, 6, n, n), lambda i: (i, 0, 0, 0)), tile],
-        out_specs=(tile, tile),
+        in_specs=[pl.BlockSpec(memory_space=pl.ANY)] * 2,
+        out_specs=(pl.BlockSpec(memory_space=pl.ANY),) * 2,
+        scratch_shapes=[pltpu.VMEM(blocks.shape, BF16), whole, whole, whole, dma((2, 12)), dma((2,))],
+        compiler_params=pltpu.CompilerParams(vmem_limit_bytes=32 * 1024 * 1024),
     )(blocks, statistic)
 
 

time: 154 us -> 157 us (1.019)
  Pallas kernels: 153 us -> 155 us
  local copies, waits for them, and re-layouts: 0 us -> 1.67 us
    pallas_call x1, Pallas kernels: 10.3 us -> 12.7 us  [shards(): pl.pallas_call(finish, out_shape=(shape, shape), in_specs=[pl.BlockSpec(m...]
    unnamed x0 -> x6, local copies, waits for them, and re-layouts: none -> 1.67 us
where the time goes in v5:
time: 157 us
  Pallas kernels  155 us (99%)
  local copies, waits for them, and re-layouts  1.67 us (1%)
    pallas_call x1, Pallas kernels, gather_blocks(): pl.pallas_call(kernel, out_shape=jax.ShapeDtypeStruct((12, 6, bs, bs), BF...  142 us
    pallas_call x1, Pallas kernels, shards(): pl.pallas_call(finish, out_shape=(shape, shape), in_specs=[pl.BlockSpec(m...  12.7 us

profile of v5, /device:TPU:9, one launch (start us, length us, event | category | flops | bytes accessed | tf_op | source)
XLA Modules:
  0.0 157.3 jit_solution(11959990424766549078)
XLA Ops:
  0.6 0.0 slice-start
  0.6 0.0 slice-start.1
  0.7 142.0 %shard_map.41.blocks = bf16[12,6,128,128]{3,2,1,0:T(8,128)(2,1)} custom-call(bf16[2,2,128,6144]{3,2,1,0:T(8,128)(2,1)} %bitcast.3), custom_call_target="tpu_custom_call" | custom-call | tf_op jit(solution)/shard_map/pallas_call | solution.py:414
  142.7 0.0 slice-done
  142.7 0.0 slice-done.1
  142.7 0.0 copy-start
  142.7 1.7 %copy-done = bf16[12,6,128,128]{3,2,1,0:T(8,128)(2,1)S(1)} copy-done((bf16[12,6,128,128]{3,2,1,0:T(8,128)(2,1)S(1)}, bf16[12,6,128,128]{3,2,1,0:T(8,128)(2,1)}, u32[]{:S(2)}) %copy-start) | copy-done | bytes 2359320
  144.4 12.7 %shard_map.42 = (f32[1536,768]{1,0:T(8,128)}, f32[1536,768]{1,0:T(8,128)}) custom-call(bf16[12,6,128,128]{3,2,1,0:T(8,128)(2,1)S(1)} %copy-done, f32[1536,768]{1,0:T(8,128)S(1)} %bitcast.2), custom_call_target="tpu_custom_call" | custom-call | tf_op jit(solution)/shard_map/pallas_call | solution.py:479
  (1 shorter events, 0.0 us)
Async XLA Ops:
  0.6 142.1 %slice-start = ((s8[4718592]{0:T(1024)(128)(4,1)}), s8[4194304]{0:T(1024)(128)(4,1)S(1)}, s32[]{:S(2)}) async-start(s8[4718592]{0:T(1024)(128)(4,1)} %bitcast.1), calls=%async_computation | async-start | bytes 8388608
  0.6 142.1 %slice-start.1 = ((s8[4718592]{0:T(1024)(128)(4,1)}), s8[524288]{0:T(1024)(128)(4,1)S(1)}, s32[]{:S(2)}) async-start(s8[4718592]{0:T(1024)(128)(4,1)} %bitcast.1), calls=%async_computation.1 | async-start | bytes 1048576
  142.7 1.7 %copy-start = (bf16[12,6,128,128]{3,2,1,0:T(8,128)(2,1)S(1)}, bf16[12,6,128,128]{3,2,1,0:T(8,128)(2,1)}, u32[]{:S(2)}) copy-start(bf16[12,6,128,128]{3,2,1,0:T(8,128)(2,1)} %shard_map.41.blocks) | copy-start | bytes 7077892

commit v6 on v5

--- a/solution.py
+++ b/solution.py
@@ -184,10 +184,16 @@
         four = sline.at[0 : 4 * q, cols(c)]
         rcopy(four, four, csend.at[9], crecv.at[9, c], sib).wait_recv()
 
+    barrier = pltpu.get_barrier_semaphore()
+    around = (sib, xp, xm, yp, ym, zp, zm)
+    for other in around:
+        pl.semaphore_signal(barrier, inc=1, device_id=other, device_id_type=MESH)
     for c in range(CHUNKS):
         load(c)
+    own[...] = jnp.zeros_like(own)
+    pl.semaphore_wait(barrier, len(around))
+    for c in range(CHUNKS):
         swap(c)
-    own[...] = jnp.zeros_like(own)
 
     def gather_step(step):
         c = step
@@ -342,19 +348,15 @@
             r.result(put)
         exchange(n)
 
-    plan = []
+    rounds = {}
     for n in range(STAGES):
-        for after, what in ((0, begin), (1, pass1), (2.3, reduce1), (3.1, pass2), (3.9, reduce2)):
-            plan.append((n + 5 + after, n, what))
-    plan.sort(key=lambda item: item[:2])
-    steps = CHUNKS + 4
-    for step in range(steps):
+        lags = (1, 3, 4, 0, 5) if n < 7 else (1, 2, 3, 0, 4)
+        for place, (lag, what) in enumerate(zip(lags, (pass1, reduce1, pass2, begin, reduce2))):
+            rounds.setdefault(n + 5 + lag, []).append((place, n, what))
+    for step in range(max(rounds) + 1):
         gather_step(step)
-        while plan and plan[0][0] <= step:
-            _, n, what = plan.pop(0)
+        for _, n, what in sorted(rounds.get(step, ()), key=lambda item: item[:2]):
             what(n)
-    for _, n, what in plan:
-        what(n)
 
     def sent(n, ref):
         rcopy(ref, ref, csend.at[n], crecv.at[0, 0], sib).wait_send()
@@ -425,7 +427,7 @@
             vm((TOTAL, b4, bs), BF16), vm((12, 6, bs, bs), BF16), vm((TOTAL, 4, b4, bs), BF16),
             dma((CHUNKS,)), dma((10,)), dma((10, CHUNKS)), dma((2, 2)), dma((2, subs, 3)), dma((2,)), dma((2,)),
         ],
-        compiler_params=pltpu.CompilerParams(has_side_effects=True, vmem_limit_bytes=56 * 1024 * 1024),
+        compiler_params=pltpu.CompilerParams(collective_id=0, has_side_effects=True, vmem_limit_bytes=56 * 1024 * 1024),
     )(grad.reshape(2, 2, q, d))
 
 
@@ -451,19 +453,13 @@
     def _(i):
         for cp in reads(i):
             cp.wait()
+        rows = (band(i), slice(None))
         for j in range(6):
             at = (band(i), slice(j * n, (j + 1) * n))
-
-            @pl.when(i >= col0 + j)
-            def _():
-                gr[at] = ub[i, j].astype(F32)
-
-            @pl.when(i < col0 + j)
-            def _():
-                gr[at] = ub[i, j].astype(F32).T
-
-        rows = (band(i), slice(None))
-        fo[rows] = 0.95 * st[rows] + 0.05 * gr[rows]
+            block = ub[i, j].astype(F32)
+            value = jnp.where(i >= col0 + j, block, block.T)
+            gr[at] = value
+            fo[at] = 0.95 * st[at] + 0.05 * value
         pltpu.make_async_copy(gr.at[rows], gram.at[rows], outsem.at[0]).start()
         pltpu.make_async_copy(fo.at[rows], following.at[rows], outsem.at[1]).start()
 
@@ -482,7 +478,7 @@
         in_specs=[pl.BlockSpec(memory_space=pl.ANY)] * 2,
         out_specs=(pl.BlockSpec(memory_space=pl.ANY),) * 2,
         scratch_shapes=[pltpu.VMEM(blocks.shape, BF16), whole, whole, whole, dma((2, 12)), dma((2,))],
-        compiler_params=pltpu.CompilerParams(vmem_limit_bytes=32 * 1024 * 1024),
+        compiler_params=pltpu.CompilerParams(vmem_limit_bytes=60 * 1024 * 1024),
     )(blocks, statistic)
 
 

time: 157 us -> 137 us (0.87)
  Pallas kernels: 155 us -> 136 us
  local copies, waits for them, and re-layouts: 1.67 us -> 0 us
    pallas_call x1, Pallas kernels: 142 us -> 130 us  [gather_blocks(): pl.pallas_call(kernel, out_shape=jax.ShapeDtypeStruct((12, 6, bs, bs), BF...]
    pallas_call x1, Pallas kernels: 12.7 us -> 6.45 us  [shards(): pl.pallas_call(finish, out_shape=(shape, shape), in_specs=[pl.BlockSpec(m...]
    unnamed x6 -> x0, local copies, waits for them, and re-layouts: 1.67 us -> none
where the time goes in v6:
time: 137 us
  Pallas kernels  136 us (99%)
    pallas_call x1, Pallas kernels, gather_blocks(): pl.pallas_call(kernel, out_shape=jax.ShapeDtypeStruct((12, 6, bs, bs), BF...  130 us
    pallas_call x1, Pallas kernels, shards(): pl.pallas_call(finish, out_shape=(shape, shape), in_specs=[pl.BlockSpec(m...  6.45 us

profile of v6, /device:TPU:9, one launch (start us, length us, event | category | flops | bytes accessed | tf_op | source)
XLA Modules:
  0.0 136.8 jit_solution(10620749615615394067)
XLA Ops:
  0.6 129.6 %shard_map.41.blocks = bf16[12,6,128,128]{3,2,1,0:T(8,128)(2,1)} custom-call(bf16[2,2,128,6144]{3,2,1,0:T(8,128)(2,1)} %bitcast.1), custom_call_target="tpu_custom_call" | custom-call | tf_op jit(solution)/shard_map/pallas_call | solution.py:416
  130.2 6.4 %shard_map.42 = (f32[1536,768]{1,0:T(8,128)}, f32[1536,768]{1,0:T(8,128)}) custom-call(bf16[12,6,128,128]{3,2,1,0:T(8,128)(2,1)} %shard_map.41.blocks, f32[1536,768]{1,0:T(8,128)} %statistic.1), custom_call_target="tpu_custom_call" | custom-call | tf_op jit(solution)/shard_map/pallas_call | solution.py:475

commit v7 on v6

--- a/solution.py
+++ b/solution.py
@@ -27,6 +27,10 @@
 
 
 TOTAL = first(STAGES)
+
+
+def block_of(i, stage):
+    return STAGES * i + mod(stage + 6 * lax.div(i, 2), STAGES)
 
 
 def mod(a, n):
@@ -86,6 +90,29 @@
                 put(m, self.add(self.i, m) + (near[m].astype(F32) + got[m].astype(F32)))
 
 
+class Spread:
+    def __init__(self, i, others, span, src, add, buf, send, recv):
+        a, b = span
+        self.i, self.add, self.buf, self.span = i, add, buf, span
+        self.copies = [
+            rcopy(src(mod(i + j, 4), a, b), buf.at[j - 1, a:b], send, recv, other) for j, other in zip((2, 1, 3), others)
+        ]
+        landed = buf.at[:, a:b]
+        self.landed = rcopy(landed, landed, send, recv, others[0])
+
+    def start(self):
+        for c in self.copies:
+            c.start()
+
+    def result(self, put):
+        self.landed.wait_recv()
+
+        @pl.loop(*self.span)
+        def _(m):
+            theirs = (self.buf[0, m].astype(F32) + self.buf[1, m].astype(F32)) + self.buf[2, m].astype(F32)
+            put(m, self.add(self.i, m) + theirs)
+
+
 def kernel(
     g, out, gown, gsib, psend, zrel, zrec, sline, own, t, l1, l2, xf, xb, o, u, spare,
     lsem, csend, crecv, rsend, rrecv, fsem, dsem,
@@ -107,6 +134,8 @@
     yp, ym = dev(x, mod(y + 1, 4), z, k), dev(x, mod(y + 3, 4), z, k)
     xp, xm = dev(mod(x + 1, 4), y, z, k), dev(mod(x + 3, 4), y, z, k)
 
+    xpp, zpp = dev(mod(x + 2, 4), y, z, k), dev(x, y, mod(z + 2, 4), k)
+
     def cols(c):
         return slice(STARTS[c] * bs, (STARTS[c] + WIDTHS[c]) * bs)
 
@@ -114,7 +143,7 @@
         return pl.ds(pl.multiple_of(i * q, q), q)
 
     def strided(c):
-        return [(pl.ds((c + STAGES * i) * bs, bs), pl.ds((4 * c + i) * bs, bs)) for i in range(4)]
+        return [(pl.ds((STAGES * i + (c + 6 * (i // 2)) % STAGES) * bs, bs), pl.ds((4 * c + i) * bs, bs)) for i in range(4)]
 
     def load(c):
         for there, here in strided(c):
@@ -274,13 +303,12 @@
                 l1.at[0:2],
                 rsend.at[0], rrecv.at[0, used],
             ))
-            twos.append(Ring(
-                *two, (a, b),
+            across = (zpp if x_first else xpp, two[1], two[2])
+            twos.append(Spread(
+                two[0], across, (a, b),
                 lambda v, a, b: xb.at[a:b, quarter(v), :],
                 lambda v, m: xf[m, quarter(v), :],
-                [l2.at[i] for i in range(4)],
-                l2.at[0:2],
-                rsend.at[1], rrecv.at[1, used],
+                l2, rsend.at[1, 0], rrecv.at[1, used, 0],
             ))
             used += 1
         rings1.append(ones)
@@ -289,12 +317,12 @@
     def exchange(n):
         for a, b, x_first in parts[n]:
             p1, p2 = (x, z) if x_first else (z, x)
-            rblk = n + STAGES * p1
+            rblk = block_of(p1, n)
 
             def one(f, up, side):
                 m = f - first(n)
                 stage = 2 * m + k
-                cblk = stage + STAGES * turn
+                cblk = block_of(turn, stage)
                 wanted = (stage <= n) if side == 0 else (stage < n)
                 rr, cc = (rblk, cblk) if side == 0 else (cblk, rblk)
                 tx, tc = lax.div(rr, 12), lax.div(cc, 6)
@@ -336,10 +364,6 @@
             r.result(put)
             r2.start()
 
-    def pass2(n):
-        for r in rings2[n]:
-            r.pass_on()
-
     def reduce2(n):
         def put(m, v):
             o[m] = v.astype(BF16)
@@ -350,8 +374,8 @@
 
     rounds = {}
     for n in range(STAGES):
-        lags = (1, 3, 4, 0, 5) if n < 7 else (1, 2, 3, 0, 4)
-        for place, (lag, what) in enumerate(zip(lags, (pass1, reduce1, pass2, begin, reduce2))):
+        lags = (0, 1, 3, 4) if n < 7 else (0, 1, 2, 3)
+        for place, (lag, what) in enumerate(zip(lags, (begin, pass1, reduce1, reduce2))):
             rounds.setdefault(n + 5 + lag, []).append((place, n, what))
     for step in range(max(rounds) + 1):
         gather_step(step)
@@ -371,10 +395,10 @@
         sent(n, zrel.at[0])
 
     ups = sum((hi - lo + 1) // 2 for ps in parts for lo, hi, _ in ps)
-    for level, ref in ((0, l1), (1, l2)):
-        for half_, blocks in ((0, ups), (1, TOTAL - ups)):
-            done = ref.at[0:3, 0:blocks]
-            rcopy(done, done, rsend.at[level, half_], rrecv.at[0, 0, 0], sib).wait_send()
+    for half_, blocks in ((0, ups), (1, TOTAL - ups)):
+        done = l1.at[0:3, 0:blocks]
+        rcopy(done, done, rsend.at[0, half_], rrecv.at[0, 0, 0], sib).wait_send()
+    rcopy(l2, l2, rsend.at[1, 0], rrecv.at[0, 0, 0], sib).wait_send()
 
     sized = (l1.at[0, 0:39], l1.at[0, 0:33])
     for core in (0, 1):
@@ -387,7 +411,7 @@
     @pl.loop(0, 12)
     def _(i):
         for j in range(6):
-            direct = i >= 6 * mod(col, 2) + j
+            direct = mod(i + 6 * lax.div(x, 2), 12) >= 6 * mod(col + zl, 2) + j
             from_me = jnp.where(direct, j % 2, mod(i, 2)) == k
 
             @pl.when(from_me)
@@ -422,7 +446,7 @@
             vm((2, q, d), BF16), vm((2, q, d), BF16), vm((q, d), BF16),
             vm((2, q // 2, d), BF16), vm((2, q // 2, d), BF16),
             vm((8 * q, d), BF16), vm((8 * q, d // 8), BF16), vm((TOTAL, 4, bs, bs), BF16),
-            vm((4, TOTAL, bs, bs), BF16), vm((4, TOTAL, b4, bs), BF16),
+            vm((4, TOTAL, bs, bs), BF16), vm((3, TOTAL, b4, bs), BF16),
             vm((TOTAL, bs, bs), F32), vm((TOTAL, bs, bs), BF16),
             vm((TOTAL, b4, bs), BF16), vm((12, 6, bs, bs), BF16), vm((TOTAL, 4, b4, bs), BF16),
             dma((CHUNKS,)), dma((10,)), dma((10, CHUNKS)), dma((2, 2)), dma((2, subs, 3)), dma((2,)), dma((2,)),
@@ -433,7 +457,9 @@
 
 def finish(blocks, statistic, gram, following, ub, st, gr, fo, insem, outsem):
     n = ub.shape[-1]
-    col0 = 6 * mod(lax.axis_index("col"), 2)
+    col = lax.axis_index("col")
+    col0 = 6 * mod(col + lax.div(col, 4), 2)
+    row0 = 6 * lax.div(lax.axis_index("row"), 2)
 
     def band(i):
         return pl.ds(pl.multiple_of(i * n, n), n)
@@ -457,7 +483,7 @@
         for j in range(6):
             at = (band(i), slice(j * n, (j + 1) * n))
             block = ub[i, j].astype(F32)
-            value = jnp.where(i >= col0 + j, block, block.T)
+            value = jnp.where(mod(i + row0, 12) >= col0 + j, block, block.T)
             gr[at] = value
             fo[at] = 0.95 * st[at] + 0.05 * value
         pltpu.make_async_copy(gr.at[rows], gram.at[rows], outsem.at[0]).start()

time: 137 us -> 134 us (0.978)
  Pallas kernels: 136 us -> 133 us
    pallas_call x1, Pallas kernels: 130 us -> 126 us  [gather_blocks(): pl.pallas_call(kernel, out_shape=jax.ShapeDtypeStruct((12, 6, bs, bs), BF...]
where the time goes in v7:
time: 134 us
  Pallas kernels  133 us (99%)
    pallas_call x1, Pallas kernels, gather_blocks(): pl.pallas_call(kernel, out_shape=jax.ShapeDtypeStruct((12, 6, bs, bs), BF...  126 us
    pallas_call x1, Pallas kernels, shards(): pl.pallas_call(finish, out_shape=(shape, shape), in_specs=[pl.BlockSpec(m...  6.45 us

profile of v7, /device:TPU:9, one launch (start us, length us, event | category | flops | bytes accessed | tf_op | source)
XLA Modules:
  0.0 133.7 jit_solution(9113982276886128154)
XLA Ops:
  0.6 126.5 %shard_map.41.blocks = bf16[12,6,128,128]{3,2,1,0:T(8,128)(2,1)} custom-call(bf16[2,2,128,6144]{3,2,1,0:T(8,128)(2,1)} %bitcast.1), custom_call_target="tpu_custom_call" | custom-call | tf_op jit(solution)/shard_map/pallas_call | solution.py:440
  127.1 6.5 %shard_map.42 = (f32[1536,768]{1,0:T(8,128)}, f32[1536,768]{1,0:T(8,128)}) custom-call(bf16[12,6,128,128]{3,2,1,0:T(8,128)(2,1)} %shard_map.41.blocks, f32[1536,768]{1,0:T(8,128)} %statistic.1), custom_call_target="tpu_custom_call" | custom-call | tf_op jit(solution)/shard_map/pallas_call | solution.py:501

commit v8 on v7

--- a/solution.py
+++ b/solution.py
@@ -377,10 +377,17 @@
         lags = (0, 1, 3, 4) if n < 7 else (0, 1, 2, 3)
         for place, (lag, what) in enumerate(zip(lags, (begin, pass1, reduce1, reduce2))):
             rounds.setdefault(n + 5 + lag, []).append((place, n, what))
-    for step in range(max(rounds) + 1):
+    final = CHUNKS + 3
+    for step in range(final):
         gather_step(step)
         for _, n, what in sorted(rounds.get(step, ()), key=lambda item: item[:2]):
             what(n)
+    gather_step(final)
+    for what, n in (
+        (begin, 10), (pass1, 9), (reduce1, 8), (begin, 11), (reduce1, 9), (pass1, 10), (reduce2, 6), (reduce2, 7),
+        (pass1, 11), (reduce2, 8), (reduce1, 10), (reduce2, 9), (reduce1, 11), (reduce2, 10), (reduce2, 11),
+    ):
+        what(n)
 
     def sent(n, ref):
         rcopy(ref, ref, csend.at[n], crecv.at[0, 0], sib).wait_send()
@@ -416,7 +423,8 @@
 
             @pl.when(from_me)
             def _():
-                rcopy(u.at[i, j], u.at[i, j], dsem.at[0], dsem.at[1], sib).start()
+                rcopy(u.at[i, j], out.at[i, j], dsem.at[0], dsem.at[1], sib).start()
+                pltpu.make_async_copy(u.at[i, j], out.at[i, j], lsem.at[0]).start()
 
     for core in (0, 1):
 
@@ -424,10 +432,7 @@
         def _():
             rcopy(sized[1 - core], sized[1 - core], dsem.at[0], dsem.at[1], sib).wait_recv()
             rcopy(sized[core], sized[core], dsem.at[0], dsem.at[1], sib).wait_send()
-
-    whole_out = pltpu.make_async_copy(u, out, lsem.at[0])
-    whole_out.start()
-    whole_out.wait()
+            pltpu.make_async_copy(sized[core], sized[core], lsem.at[0]).wait()
 
 
 def gather_blocks(grad):

time: 134 us -> 132 us (0.985)
  Pallas kernels: 133 us -> 131 us
    pallas_call x1, Pallas kernels: 126 us -> 125 us  [gather_blocks(): pl.pallas_call(kernel, out_shape=jax.ShapeDtypeStruct((12, 6, bs, bs), BF...]
where the time goes in v8:
time: 132 us
  Pallas kernels  131 us (99%)
    pallas_call x1, Pallas kernels, gather_blocks(): pl.pallas_call(kernel, out_shape=jax.ShapeDtypeStruct((12, 6, bs, bs), BF...  125 us
    pallas_call x1, Pallas kernels, shards(): pl.pallas_call(finish, out_shape=(shape, shape), in_specs=[pl.BlockSpec(m...  6.45 us

profile of v8, /device:TPU:9, one launch (start us, length us, event | category | flops | bytes accessed | tf_op | source)
XLA Modules:
  0.0 132.3 jit_solution(5798003395571388850)
XLA Ops:
  0.6 125.0 %shard_map.41.blocks = bf16[12,6,128,128]{3,2,1,0:T(8,128)(2,1)} custom-call(bf16[2,2,128,6144]{3,2,1,0:T(8,128)(2,1)} %bitcast.1), custom_call_target="tpu_custom_call" | custom-call | tf_op jit(solution)/shard_map/pallas_call | solution.py:445
  125.7 6.5 %shard_map.42 = (f32[1536,768]{1,0:T(8,128)}, f32[1536,768]{1,0:T(8,128)}) custom-call(bf16[12,6,128,128]{3,2,1,0:T(8,128)(2,1)} %shard_map.41.blocks, f32[1536,768]{1,0:T(8,128)} %statistic.1), custom_call_target="tpu_custom_call" | custom-call | tf_op jit(solution)/shard_map/pallas_call | solution.py:506

commit v9 on v8

--- a/solution.py
+++ b/solution.py
@@ -29,8 +29,18 @@
 TOTAL = first(STAGES)
 
 
+def halved(v):
+    return v // 2 if isinstance(v, int) else lax.div(v, 2)
+
+
 def block_of(i, stage):
-    return STAGES * i + mod(stage + 6 * lax.div(i, 2), STAGES)
+    upper = (halved(stage) + halved(i)) % 2 if isinstance(i, int) else mod(halved(stage) + halved(i), 2)
+    odd = stage % 2 if isinstance(stage, int) else mod(stage, 2)
+    return STAGES * i + 6 * upper + 2 * halved(halved(stage)) + odd
+
+
+def stage_of(i, upper, place):
+    return 4 * halved(place) + 2 * mod(upper + halved(i), 2) + (place % 2 if isinstance(place, int) else mod(place, 2))
 
 
 def mod(a, n):
@@ -143,7 +153,7 @@
         return pl.ds(pl.multiple_of(i * q, q), q)
 
     def strided(c):
-        return [(pl.ds((STAGES * i + (c + 6 * (i // 2)) % STAGES) * bs, bs), pl.ds((4 * c + i) * bs, bs)) for i in range(4)]
+        return [(pl.ds(block_of(i, c) * bs, bs), pl.ds((4 * c + i) * bs, bs)) for i in range(4)]
 
     def load(c):
         for there, here in strided(c):
@@ -260,7 +270,10 @@
             share(2, c).start()
 
     turn = 2 * mod(y, 2) + lax.div(y, 2)
-    strip = 4 * k + turn
+
+    def quarter_of(m):
+        return mod(turn + 2 * m + 2 * k, 4)
+
 
     def tiles(n):
         for c in range(CHUNKS):
@@ -270,7 +283,7 @@
 
         @pl.when(k == n % 2)
         def _():
-            mine = pl.ds(pl.multiple_of((8 * last + strip) * bs, bs), bs)
+            mine = pl.ds(pl.multiple_of((4 * n + quarter_of(last)) * bs, bs), bs)
             own[:, last * bs : (last + 1) * bs] = sline[:, mine]
 
         lhs = sline[:, 4 * n * bs : 4 * (n + 1) * bs]
@@ -322,7 +335,7 @@
             def one(f, up, side):
                 m = f - first(n)
                 stage = 2 * m + k
-                cblk = block_of(turn, stage)
+                cblk = block_of(quarter_of(m), stage)
                 wanted = (stage <= n) if side == 0 else (stage < n)
                 rr, cc = (rblk, cblk) if side == 0 else (cblk, rblk)
                 tx, tc = lax.div(rr, 12), lax.div(cc, 6)
@@ -418,7 +431,7 @@
     @pl.loop(0, 12)
     def _(i):
         for j in range(6):
-            direct = mod(i + 6 * lax.div(x, 2), 12) >= 6 * mod(col + zl, 2) + j
+            direct = stage_of(x, lax.div(i, 6), mod(i, 6)) >= stage_of(halved(col), mod(col, 2), j)
             from_me = jnp.where(direct, j % 2, mod(i, 2)) == k
 
             @pl.when(from_me)
@@ -463,8 +476,7 @@
 def finish(blocks, statistic, gram, following, ub, st, gr, fo, insem, outsem):
     n = ub.shape[-1]
     col = lax.axis_index("col")
-    col0 = 6 * mod(col + lax.div(col, 4), 2)
-    row0 = 6 * lax.div(lax.axis_index("row"), 2)
+    row = lax.axis_index("row")
 
     def band(i):
         return pl.ds(pl.multiple_of(i * n, n), n)
@@ -488,7 +500,8 @@
         for j in range(6):
             at = (band(i), slice(j * n, (j + 1) * n))
             block = ub[i, j].astype(F32)
-            value = jnp.where(mod(i + row0, 12) >= col0 + j, block, block.T)
+            direct = stage_of(row, lax.div(i, 6), mod(i, 6)) >= stage_of(halved(col), mod(col, 2), j)
+            value = jnp.where(direct, block, block.T)
             gr[at] = value
             fo[at] = 0.95 * st[at] + 0.05 * value
         pltpu.make_async_copy(gr.at[rows], gram.at[rows], outsem.at[0]).start()

time: 132 us -> 118 us (0.89)
  Pallas kernels: 131 us -> 116 us
    pallas_call x1, Pallas kernels: 125 us -> 110 us  [gather_blocks(): pl.pallas_call(kernel, out_shape=jax.ShapeDtypeStruct((12, 6, bs, bs), BF...]
where the time goes in v9:
time: 118 us; the launch traced here: 117 us
  Pallas kernels  116 us (98%)
    pallas_call x1, Pallas kernels, gather_blocks(): pl.pallas_call(kernel, out_shape=jax.ShapeDtypeStruct((12, 6, bs, bs), BF...  110 us
    pallas_call x1, Pallas kernels, shards(): pl.pallas_call(finish, out_shape=(shape, shape), in_specs=[pl.BlockSpec(m...  6.45 us

profile of v9, /device:TPU:9, one launch (start us, length us, event | category | flops | bytes accessed | tf_op | source)
XLA Modules:
  0.0 117.0 jit_solution(18278713217022174263)
XLA Ops:
  0.6 109.7 %shard_map.41.blocks = bf16[12,6,128,128]{3,2,1,0:T(8,128)(2,1)} custom-call(bf16[2,2,128,6144]{3,2,1,0:T(8,128)(2,1)} %bitcast.1), custom_call_target="tpu_custom_call" | custom-call | tf_op jit(solution)/shard_map/pallas_call | solution.py:458
  110.4 6.4 %shard_map.42 = (f32[1536,768]{1,0:T(8,128)}, f32[1536,768]{1,0:T(8,128)}) custom-call(bf16[12,6,128,128]{3,2,1,0:T(8,128)(2,1)} %shard_map.41.blocks, f32[1536,768]{1,0:T(8,128)} %statistic.1), custom_call_target="tpu_custom_call" | custom-call | tf_op jit(solution)/shard_map/pallas_call | solution.py:519

commit v10 on v9

--- a/solution.py
+++ b/solution.py
@@ -387,7 +387,7 @@
 
     rounds = {}
     for n in range(STAGES):
-        lags = (0, 1, 3, 4) if n < 7 else (0, 1, 2, 3)
+        lags = (0, 1, 3, 4) if n < 6 else (0, 1, 2, 3)
         for place, (lag, what) in enumerate(zip(lags, (begin, pass1, reduce1, reduce2))):
             rounds.setdefault(n + 5 + lag, []).append((place, n, what))
     final = CHUNKS + 3
@@ -397,8 +397,8 @@
             what(n)
     gather_step(final)
     for what, n in (
-        (begin, 10), (pass1, 9), (reduce1, 8), (begin, 11), (reduce1, 9), (pass1, 10), (reduce2, 6), (reduce2, 7),
-        (pass1, 11), (reduce2, 8), (reduce1, 10), (reduce2, 9), (reduce1, 11), (reduce2, 10), (reduce2, 11),
+        (begin, 10), (pass1, 9), (reduce1, 8), (begin, 11), (reduce2, 7), (pass1, 10), (reduce1, 9), (pass1, 11),
+        (reduce2, 8), (reduce1, 10), (reduce2, 9), (reduce1, 11), (reduce2, 10), (reduce2, 11),
     ):
         what(n)
 

time: 118 us -> 117 us (level)
  no operation moved by 1% of the time
where the time goes in v10:
time: 117 us
  Pallas kernels  116 us (99%)
    pallas_call x1, Pallas kernels, gather_blocks(): pl.pallas_call(kernel, out_shape=jax.ShapeDtypeStruct((12, 6, bs, bs), BF...  109 us
    pallas_call x1, Pallas kernels, shards(): pl.pallas_call(finish, out_shape=(shape, shape), in_specs=[pl.BlockSpec(m...  6.45 us

profile of v10, /device:TPU:9, one launch (start us, length us, event | category | flops | bytes accessed | tf_op | source)
XLA Modules:
  0.0 116.6 jit_solution(13522492390533643440)
XLA Ops:
  0.6 109.4 %shard_map.41.blocks = bf16[12,6,128,128]{3,2,1,0:T(8,128)(2,1)} custom-call(bf16[2,2,128,6144]{3,2,1,0:T(8,128)(2,1)} %bitcast.1), custom_call_target="tpu_custom_call" | custom-call | tf_op jit(solution)/shard_map/pallas_call | solution.py:458
  110.0 6.4 %shard_map.42 = (f32[1536,768]{1,0:T(8,128)}, f32[1536,768]{1,0:T(8,128)}) custom-call(bf16[12,6,128,128]{3,2,1,0:T(8,128)(2,1)} %shard_map.41.blocks, f32[1536,768]{1,0:T(8,128)} %statistic.1), custom_call_target="tpu_custom_call" | custom-call | tf_op jit(solution)/shard_map/pallas_call | solution.py:519

commit v11 on v10

--- a/solution.py
+++ b/solution.py
@@ -16,6 +16,7 @@
 STARTS = tuple(sum(WIDTHS[:i]) for i in range(len(WIDTHS)))
 CHUNKS = len(WIDTHS)
 BETA_FROM = 8
+LATE = 10
 
 
 def count(n):
@@ -41,6 +42,15 @@
 
 def stage_of(i, upper, place):
     return 4 * halved(place) + 2 * mod(upper + halved(i), 2) + (place % 2 if isinstance(place, int) else mod(place, 2))
+
+
+def landing(core, upper, late):
+    total = 0
+    for r in range(STAGES):
+        for c in range(STAGES):
+            if (c // 2) % 2 == upper and min(r, c) % 2 == core and (max(r, c) >= LATE) == late:
+                total += 1
+    return total
 
 
 def mod(a, n):
@@ -328,6 +338,7 @@
         rings2.append(twos)
 
     def exchange(n):
+        landed = fsem.at[2 if n >= LATE else 1]
         for a, b, x_first in parts[n]:
             p1, p2 = (x, z) if x_first else (z, x)
             rblk = block_of(p1, n)
@@ -346,11 +357,11 @@
 
                 @pl.when(wanted & jnp.logical_not(mine))
                 def _():
-                    rcopy(src, dst, fsem.at[0], fsem.at[1], dev(tx, ty, tz, k)).start()
+                    rcopy(src, dst, fsem.at[0], landed, dev(tx, ty, tz, k)).start()
 
                 @pl.when(wanted & mine)
                 def _():
-                    pltpu.make_async_copy(src, dst, fsem.at[1]).start()
+                    pltpu.make_async_copy(src, dst, landed).start()
                     pltpu.make_async_copy(src, spare.at[f, 2 * side + up], fsem.at[0]).start()
 
             @pl.loop(a, b)
@@ -420,24 +431,40 @@
         rcopy(done, done, rsend.at[0, half_], rrecv.at[0, 0, 0], sib).wait_send()
     rcopy(l2, l2, rsend.at[1, 0], rrecv.at[0, 0, 0], sib).wait_send()
 
+    upper = mod(col + zl, 2)
+
+    def arrived(late):
+        for core in (0, 1):
+            for part in (0, 1):
+
+                @pl.when((k == core) & (upper == part))
+                def _():
+                    ref = l1.at[0, 0 : landing(core, part, late)]
+                    rcopy(ref, ref, fsem.at[0], fsem.at[2 if late else 1], sib).wait_recv()
+
+    def swap_blocks(late):
+        @pl.loop(0, 12)
+        def _(i):
+            for j in range(6):
+                r = stage_of(x, lax.div(i, 6), mod(i, 6))
+                c = stage_of(halved(col), mod(col, 2), j)
+                from_me = jnp.where(r >= c, j % 2, mod(i, 2)) == k
+                now = (r >= LATE) | (c >= LATE)
+
+                @pl.when(from_me & (now if late else jnp.logical_not(now)))
+                def _():
+                    rcopy(u.at[i, j], out.at[i, j], dsem.at[0], dsem.at[1], sib).start()
+                    pltpu.make_async_copy(u.at[i, j], out.at[i, j], lsem.at[0]).start()
+
+    for late in (False, True):
+        arrived(late)
+        swap_blocks(late)
     sized = (l1.at[0, 0:39], l1.at[0, 0:33])
     for core in (0, 1):
 
         @pl.when(k == core)
         def _():
-            rcopy(sized[core], sized[core], fsem.at[0], fsem.at[1], sib).wait_recv()
             rcopy(sized[core], sized[core], fsem.at[0], fsem.at[1], sib).wait_send()
-
-    @pl.loop(0, 12)
-    def _(i):
-        for j in range(6):
-            direct = stage_of(x, lax.div(i, 6), mod(i, 6)) >= stage_of(halved(col), mod(col, 2), j)
-            from_me = jnp.where(direct, j % 2, mod(i, 2)) == k
-
-            @pl.when(from_me)
-            def _():
-                rcopy(u.at[i, j], out.at[i, j], dsem.at[0], dsem.at[1], sib).start()
-                pltpu.make_async_copy(u.at[i, j], out.at[i, j], lsem.at[0]).start()
 
     for core in (0, 1):
 
@@ -467,7 +494,7 @@
             vm((4, TOTAL, bs, bs), BF16), vm((3, TOTAL, b4, bs), BF16),
             vm((TOTAL, bs, bs), F32), vm((TOTAL, bs, bs), BF16),
             vm((TOTAL, b4, bs), BF16), vm((12, 6, bs, bs), BF16), vm((TOTAL, 4, b4, bs), BF16),
-            dma((CHUNKS,)), dma((10,)), dma((10, CHUNKS)), dma((2, 2)), dma((2, subs, 3)), dma((2,)), dma((2,)),
+            dma((CHUNKS,)), dma((10,)), dma((10, CHUNKS)), dma((2, 2)), dma((2, subs, 3)), dma((3,)), dma((2,)),
         ],
         compiler_params=pltpu.CompilerParams(collective_id=0, has_side_effects=True, vmem_limit_bytes=56 * 1024 * 1024),
     )(grad.reshape(2, 2, q, d))

time: 117 us -> 116 us (level)
  no operation moved by 1% of the time
where the time goes in v11:
time: 116 us
  Pallas kernels  115 us (99%)
    pallas_call x1, Pallas kernels, gather_blocks(): pl.pallas_call(kernel, out_shape=jax.ShapeDtypeStruct((12, 6, bs, bs), BF...  108 us
    pallas_call x1, Pallas kernels, shards(): pl.pallas_call(finish, out_shape=(shape, shape), in_specs=[pl.BlockSpec(m...  6.45 us

profile of v11, /device:TPU:9, one launch (start us, length us, event | category | flops | bytes accessed | tf_op | source)
XLA Modules:
  0.0 115.6 jit_solution(5404158226878324125)
XLA Ops:
  0.6 108.4 %shard_map.41.blocks = bf16[12,6,128,128]{3,2,1,0:T(8,128)(2,1)} custom-call(bf16[2,2,128,6144]{3,2,1,0:T(8,128)(2,1)} %bitcast.1), custom_call_target="tpu_custom_call" | custom-call | tf_op jit(solution)/shard_map/pallas_call | solution.py:485
  109.0 6.4 %shard_map.42 = (f32[1536,768]{1,0:T(8,128)}, f32[1536,768]{1,0:T(8,128)}) custom-call(bf16[12,6,128,128]{3,2,1,0:T(8,128)(2,1)} %shard_map.41.blocks, f32[1536,768]{1,0:T(8,128)} %statistic.1), custom_call_target="tpu_custom_call" | custom-call | tf_op jit(solution)/shard_map/pallas_call | solution.py:546
